TPU v7x, 256 devices: a whole 4x4x8 slice. The times are simulated.
256 devices in a mesh: radial: 64 (over x, z, core), phi: 4 (over y).
Axes of the slice: x: 4, y: 4, z: 8, core: 2. Of those that a mesh axis runs over, the one named last changes fastest.
Arguments:
- conserved: float32 [8, 512, 64, 128], P(None, 'radial', 'phi'), may hold values from -2.5 to 7, as said below
- core_mass: float32 [1], replicated, may hold values from 0.2 to 1
Outputs:
- advanced: float32 [8, 512, 64, 128], P(None, 'radial', 'phi')
- enclosed_mass: float32 [512], P('radial')
Inputs may be any that keep to these rules, and one draw needn't show every extreme that they name: conserved[0] (density) lies between 0.4 and 2.5; conserved[4] exceeds (conserved[1]^2 + conserved[2]^2 + conserved[3]^2)/(2 conserved[0]) by at least 0.6; the speeds |conserved[m]/conserved[0]| stay below 1; conserved[5..7] lie between 0 and conserved[0].
All inputs are finite; a program needn't handle non-finite values.
Results may differ from a plain program's by a relative error of at most 0.0003.
Values sent between devices are 32-bit elements; how exact they have to be, the bound alone decides.
A program may use at most 64 MiB of HBM per device.

v0:
```python
import math

import jax
import jax.numpy as jnp
from jax import lax
from jax.sharding import PartitionSpec as P

ADIABATIC = 4.0 / 3.0
INNER_RADIUS = 1.0
OUTER_RADIUS = 2.0
COURANT = 0.4
GRAVITY_KICK = 0.004
MINIMUM_DENSITY = 0.05
PRESSURE_FLOOR = 0.01


def from_everyone(value, axis):
    peers = lax.axis_size(axis)
    return lax.all_to_all(
        jnp.broadcast_to(value[None], (peers, *value.shape)), axis, 0, 0, tiled=True
    )


def taken_together(value, axis):
    return from_everyone(value, axis).sum(axis=0)


def combined_pairwise(pieces, combine):
    while len(jax.tree.leaves(pieces)[0]) > 1:
        pieces = jax.vmap(combine)(*(pieces[side::2] for side in (0, 1)))
    return pieces[0]


def entering(value, axis, combine, identity):
    peers, place = (lax.axis_size(axis), lax.axis_index(axis))
    passed = jnp.arange(peers) < place

    def kept(part, zero, own):
        part = jnp.where(
            passed.reshape(-1, *(1 for _ in own.shape)), part, jnp.asarray(zero, own.dtype)
        )
        return part

    pieces = from_everyone(value, axis)
    return combined_pairwise(kept(pieces, identity, value), combine)


def extended_2(value, sides, width, wrap):
    for axis, dim in sides:
        peers, length = (lax.axis_size(axis), value.shape[dim])
        up = [(i, (i + 1) % peers) for i in range(peers if wrap else peers - 1)]
        down = [(j, i) for i, j in up]
        last = lax.slice_in_dim(value, length - width, length, axis=dim)
        initial = lax.slice_in_dim(value, 0, width, axis=dim)
        before = lax.ppermute(last, axis, up)
        after = lax.ppermute(initial, axis, down)
        value = jnp.concatenate([before, value, after], axis=dim)
    return value


def step_sizes(radial_total, phi_total, theta_total):
    theta_step = math.pi / theta_total
    phi_step = 2.0 * math.pi / phi_total
    polar_width = INNER_RADIUS * math.sin(0.5 * theta_step) * phi_step
    radial_step = min(2.0 * polar_width, (OUTER_RADIUS - INNER_RADIUS) / radial_total)
    timestep = COURANT * min(radial_step, polar_width)
    return (radial_step, theta_step, phi_step, timestep)


def thermo(values):
    density = jnp.maximum(values[0], MINIMUM_DENSITY)
    kinetic = (
        0.5 * (values[1] * values[1] + values[2] * values[2] + values[3] * values[3]) / density
    )
    pressure = jnp.maximum((ADIABATIC - 1.0) * (values[4] - kinetic), PRESSURE_FLOOR * density)
    return (density, pressure)


def physical(values, component):
    density, pressure = thermo(values)
    normal = values[component] / density
    sound = jnp.sqrt(ADIABATIC * pressure / density)
    pieces = [values[which] * normal for which in range(values.shape[0])]
    pieces[component] = pieces[component] + pressure
    pieces[4] = pieces[4] + pressure * normal
    return (jnp.stack(pieces), jnp.abs(normal) + sound)


def face_flux(values, along_dim, component):
    interior = values.shape[along_dim] - 4
    neighbour_differences = lax.slice_in_dim(
        values, 1, interior + 4, axis=along_dim
    ) - lax.slice_in_dim(values, 0, interior + 3, axis=along_dim)
    below_diff = lax.slice_in_dim(neighbour_differences, 0, interior + 2, axis=along_dim)
    above_diff = lax.slice_in_dim(neighbour_differences, 1, interior + 3, axis=along_dim)
    limited = (
        0.5
        * (jnp.sign(below_diff) + jnp.sign(above_diff))
        * jnp.minimum(jnp.abs(below_diff), jnp.abs(above_diff))
    )
    left_state = lax.slice_in_dim(values, 1, interior + 2, axis=along_dim) + 0.5 * lax.slice_in_dim(
        limited, 0, interior + 1, axis=along_dim
    )
    right_state = lax.slice_in_dim(
        values, 2, interior + 3, axis=along_dim
    ) - 0.5 * lax.slice_in_dim(limited, 1, interior + 2, axis=along_dim)
    left_flux, left_signal = physical(left_state, component)
    right_flux, right_signal = physical(right_state, component)
    signal = jnp.maximum(left_signal, right_signal)
    return 0.5 * (left_flux + right_flux) - 0.5 * signal * (right_state - left_state)


def hydro_rate(extended, cell_centers, enclosed, radial_step, theta_step, phi_step, strength):
    theta_cells = extended.shape[3]
    centre_cells = extended[:, 2:-2, 2:-2, :]
    polar_padded = jnp.pad(centre_cells, ((0, 0), (0, 0), (0, 0), (2, 2)), mode="edge")
    radial_flux = face_flux(extended[:, :, 2:-2, :], 1, 1)
    polar_flux = face_flux(polar_padded, 3, 2)
    azimuth_flux = face_flux(extended[:, 2:-2, :, :], 2, 3)
    angles = (jnp.arange(theta_cells, dtype=jnp.float32) + 0.5) * theta_step
    sine_center = jnp.sin(angles)
    cosine = jnp.cos(angles)
    face_sine = jnp.sin(jnp.arange(theta_cells + 1, dtype=jnp.float32) * theta_step)
    radius = cell_centers[:, None, None]
    face_radius = jnp.concatenate(
        [cell_centers - 0.5 * radial_step, cell_centers[-1:] + 0.5 * radial_step]
    )[:, None, None]
    radial_area = face_radius * face_radius * radial_flux
    divergence = (radial_area[:, 1:] - radial_area[:, :-1]) / (radius * radius * radial_step)
    polar_area = face_sine * polar_flux
    divergence = divergence + (polar_area[..., 1:] - polar_area[..., :-1]) / (
        radius * sine_center * theta_step
    )
    divergence = divergence + (azimuth_flux[:, :, 1:] - azimuth_flux[:, :, :-1]) / (
        radius * sine_center * phi_step
    )
    density, pressure = thermo(centre_cells)
    radial_speed = centre_cells[1] / density
    polar_speed = centre_cells[2] / density
    azimuth_speed = centre_cells[3] / density
    cotangent = cosine / sine_center
    gravity_pull = strength * enclosed[:, None, None] / (radius * radius)
    source_radial = (
        2.0 * pressure + density * (polar_speed * polar_speed + azimuth_speed * azimuth_speed)
    ) / radius - density * gravity_pull
    source_polar = (
        pressure * cotangent
        + density * azimuth_speed * azimuth_speed * cotangent
        - density * radial_speed * polar_speed
    ) / radius
    source_azimuth = -density * azimuth_speed * (radial_speed + polar_speed * cotangent) / radius
    source_energy = -centre_cells[1] * gravity_pull
    nothing = jnp.zeros_like(pressure)
    source = jnp.stack(
        [
            nothing,
            source_radial,
            source_polar,
            source_azimuth,
            source_energy,
            nothing,
            nothing,
            nothing,
        ]
    )
    return source - divergence


def add_terms(earlier, later):
    return earlier + later


def body(conserved, core_mass):
    radial_rows = conserved.shape[1]
    phi_cells = conserved.shape[2]
    theta_cells = conserved.shape[3]
    radial_devices = lax.axis_size("radial")
    position = lax.axis_index("radial")
    radial_step, theta_step, phi_step, timestep = step_sizes(
        radial_rows * radial_devices, phi_cells * lax.axis_size("phi"), theta_cells
    )
    strength = GRAVITY_KICK / timestep
    first_row = position * radial_rows
    cell_centers = (
        INNER_RADIUS
        + ((first_row + jnp.arange(radial_rows, dtype=jnp.int32)).astype(jnp.float32) + 0.5)
        * radial_step
    )
    sine_center = jnp.sin((jnp.arange(theta_cells, dtype=jnp.float32) + 0.5) * theta_step)
    local_shells = jnp.dot(
        jnp.sum(conserved[0], axis=1), sine_center, precision=lax.Precision.HIGHEST
    )
    local_shells = (
        local_shells * cell_centers * cell_centers * (radial_step * theta_step * phi_step)
    )
    shells = taken_together(local_shells, "phi")
    before = entering(jnp.sum(shells), "radial", add_terms, jnp.float32(0.0))
    enclosed = core_mass[0] + before + jnp.cumsum(shells) - 0.5 * shells

    def clipped_rows(extended, halo_width):
        total_rows = extended.shape[1]
        low_rows = jnp.where(
            position == 0,
            lax.slice_in_dim(extended, halo_width, halo_width + 1, axis=1),
            lax.slice_in_dim(extended, 0, halo_width, axis=1),
        )
        high_rows = jnp.where(
            position == radial_devices - 1,
            lax.slice_in_dim(
                extended, total_rows - halo_width - 1, total_rows - halo_width, axis=1
            ),
            lax.slice_in_dim(extended, total_rows - halo_width, total_rows, axis=1),
        )
        middle = lax.slice_in_dim(extended, halo_width, total_rows - halo_width, axis=1)
        return jnp.concatenate([low_rows, middle, high_rows], axis=1)

    def extend(values):
        wedge_split_state = extended_2(values, (("phi", 2),), 2, True)
        slab_split_state = extended_2(wedge_split_state, (("radial", 1),), 2, False)
        return clipped_rows(slab_split_state, 2)

    section_one = conserved + timestep * hydro_rate(
        extend(conserved), cell_centers, enclosed, radial_step, theta_step, phi_step, strength
    )
    section_two = section_one + timestep * hydro_rate(
        extend(section_one), cell_centers, enclosed, radial_step, theta_step, phi_step, strength
    )
    advanced = 0.5 * conserved + 0.5 * section_two
    return (advanced, enclosed)


def solution(mesh):
    in_specs = (P(None, "radial", "phi", None), P())
    out_specs = (P(None, "radial", "phi", None), P("radial"))
    return jax.shard_map(body, mesh=mesh, in_specs=in_specs, out_specs=out_specs, check_vma=False)
```

profile of v0, /device:TPU:2, one launch (start us, length us, event | category | flops | bytes accessed | tf_op | source)
XLA Modules:
  0.0 79.3 jit_solution(11763445968841728372)
XLA Ops:
  0.6 1.1 %fusion.54 = (f32[8,8,2,128]{3,2,1,0:T(2,128)S(1)}, f32[8,8,2,128]{3,2,1,0:T(2,128)S(1)}) fusion(f32[8,8,16,128]{3,2,1,0:T(8,128)} %param.2), kind=kLoop, calls=%fused_computation.340 | loop fusion | bytes 262144 | tf_op jit(solution)/shard_map/slice | solution.py:53
  1.8 1.7 %collective-permute-start = (f32[8,8,2,128]{3,1,2,0:T(8,128)S(1)}, f32[8,8,2,128]{3,1,2,0:T(8,128)S(1)}, u32[]{:S(2)}, u32[]{:S(2)}) collective-permute-start(f32[8,8,2,128]{3,1,2,0:T(8,128)S(1)} %copy.721), channel_id=1, source_target_pairs={{0,1},{1,2},{2,3},{3,0},{4,5},{5,6},{6,7},{7,4},{8,9},{9,10},{10,1... | collective-permute-start | bytes 196616 | tf_op jit(solution)/shard_map/ppermute | solution.py:55
  3.5 1.7 %collective-permute-start.1 = (f32[8,8,2,128]{3,1,2,0:T(8,128)S(1)}, f32[8,8,2,128]{3,1,2,0:T(8,128)S(1)}, u32[]{:S(2)}, u32[]{:S(2)}) collective-permute-start(f32[8,8,2,128]{3,1,2,0:T(8,128)S(1)} %copy.722), channel_id=1, source_target_pairs={{1,0},{2,1},{3,2},{0,3},{5,4},{6,5},{7,6},{4,7},{9,8},{10,9},{11,1... | collective-permute-start | bytes 196616 | tf_op jit(solution)/shard_map/ppermute | solution.py:56
  5.1 0.9 %slice_reduce_fusion.2 = f32[8,128]{1,0:T(8,128)S(1)} fusion(f32[8,8,16,128]{3,2,1,0:T(8,128)} %param.2), kind=kLoop, calls=%fused_computation.312 | loop fusion | flops 15360 | bytes 69632
  6.0 0.2 fusion.2
  6.1 0.6 broadcast_in_dim.45
  6.7 3.3 %all-to-all-start = ((f32[4,1,8]{2,1,0:T(1,128)}), f32[4,1,8]{2,1,0:T(1,128)S(1)}, u32[]{:S(2)}, u32[]{:S(2)}) async-start(f32[4,1,8]{2,1,0:T(1,128)} %broadcast_in_dim.45), calls=%async_computation | async-start | bytes 4096 | tf_op jit(solution)/shard_map/all_to_all | solution.py:19
  10.0 0.2 fusion.53
  10.4 0.6 slice.760
  11.0 0.4 copy.723
  11.4 0.4 copy.724
  11.9 0.2 reshape.178
  12.1 0.2 reshape.179
  12.3 0.5 pad_maximum_fusion.6
  12.8 0.3 slice_subtract_fusion.1
  13.1 0.7 minimum_multiply_fusion.1
  13.9 0.8 fusion.6
  14.6 0.2 multiply_bitcast_fusion.1
  16.1 0.5 subtract_multiply_fusion.1
  16.7 0.6 fusion.48
  17.3 1.3 %broadcast_in_dim.46 = f32[64,1,1]{2,1,0:T(1,128)} broadcast(f32[]{:T(128)} %get-tuple-element.18), dimensions={} | broadcast | bytes 260 | tf_op jit(solution)/shard_map/broadcast_in_dim | solution.py:20
  18.6 12.0 %all-to-all-start.1 = ((f32[64,1,1]{2,1,0:T(1,128)}), f32[64,1,1]{2,1,0:T(1,128)S(1)}, u32[]{:S(2)}, u32[]{:S(2)}) async-start(f32[64,1,1]{2,1,0:T(1,128)} %broadcast_in_dim.46), calls=%async_computation.1 | async-start | bytes 65536 | tf_op jit(solution)/shard_map/all_to_all | solution.py:19
  31.2 0.2 reduce-window.7
  31.4 7.7 %all-to-all-done.1 = f32[64,1,1]{2,1,0:T(1,128)S(1)} async-done(((f32[64,1,1]{2,1,0:T(1,128)}), f32[64,1,1]{2,1,0:T(1,128)S(1)}, u32[]{:S(2)}, u32[]{:S(2)}) %all-to-all-start.1) | async-done | bytes 288 | tf_op jit(solution)/shard_map/all_to_all | solution.py:19
  39.1 0.6 reduce.4
  39.8 0.1 slice.749
  40.8 0.6 fusion.55
  42.7 0.5 multiply_divide_fusion
  44.0 2.8 %collective-permute-start.3 = (f32[8,2,20,128]{3,0,2,1:T(8,128)S(1)}, f32[8,2,20,128]{3,0,2,1:T(8,128)S(1)}, u32[]{:S(2)}, u32[]{:S(2)}) collective-permute-start(f32[8,2,20,128]{3,0,2,1:T(8,128)S(1)} %copy.686), channel_id=1, source_target_pairs={{4,0},{8,4},{12,8},{16,12},{20,16},{24,20},{28,24},{32,28},{36,32}... | collective-permute-start | bytes 491528 | tf_op jit(solution)/shard_map/ppermute | solution.py:56
  46.9 2.1 %collective-permute-start.2 = (f32[8,2,20,128]{3,0,2,1:T(8,128)S(1)}, f32[8,2,20,128]{3,0,2,1:T(8,128)S(1)}, u32[]{:S(2)}, u32[]{:S(2)}) collective-permute-start(f32[8,2,20,128]{3,0,2,1:T(8,128)S(1)} %copy.682), channel_id=1, source_target_pairs={{0,4},{4,8},{8,12},{12,16},{16,20},{20,24},{24,28},{28,32},{32,36}... | collective-permute-start | bytes 491528 | tf_op jit(solution)/shard_map/ppermute | solution.py:55
  49.0 0.6 minimum_multiply_fusion.3
  49.5 0.3 fusion.10
  49.8 0.2 multiply_bitcast_fusion.3
  50.4 0.2 multiply_subtract_fusion.1
  50.7 4.9 %collective-permute-done.2 = f32[8,2,20,128]{3,0,2,1:T(8,128)S(1)} collective-permute-done((f32[8,2,20,128]{3,0,2,1:T(8,128)S(1)}, f32[8,2,20,128]{3,0,2,1:T(8,128)S(1)}, u32[]{:S(2)}, u32[]{:S(2)}) %collective-permute-start.2) | collective-permute-done | bytes 163872 | tf_op jit(solution)/shard_map/ppermute | solution.py:55
  55.6 0.2 pad_maximum_fusion
  55.9 0.3 minimum_multiply_fusion.5
  56.3 0.1 multiply_bitcast_fusion.5
  56.8 0.2 subtract_multiply_fusion.3
  57.0 0.4 fusion.28
  57.4 0.5 slice_reduce_fusion.1
  57.9 2.1 %collective-permute-start.4 = (f32[8,8,2,128]{3,1,2,0:T(8,128)S(1)}, f32[8,8,2,128]{3,1,2,0:T(8,128)S(1)}, u32[]{:S(2)}, u32[]{:S(2)}) collective-permute-start(f32[8,8,2,128]{3,1,2,0:T(8,128)S(1)} %copy.696), channel_id=1, source_target_pairs={{0,1},{1,2},{2,3},{3,0},{4,5},{5,6},{6,7},{7,4},{8,9},{9,10},{10,1... | collective-permute-start | bytes 196616 | tf_op jit(solution)/shard_map/ppermute | solution.py:55
  60.0 1.3 %collective-permute-start.5 = (f32[8,8,2,128]{3,1,2,0:T(8,128)S(1)}, f32[8,8,2,128]{3,1,2,0:T(8,128)S(1)}, u32[]{:S(2)}, u32[]{:S(2)}) collective-permute-start(f32[8,8,2,128]{3,1,2,0:T(8,128)S(1)} %copy.697), channel_id=1, source_target_pairs={{1,0},{2,1},{3,2},{0,3},{5,4},{6,5},{7,6},{4,7},{9,8},{10,9},{11,1... | collective-permute-start | bytes 196616 | tf_op jit(solution)/shard_map/ppermute | solution.py:56
  61.4 0.2 reshape.180
  61.5 0.2 reshape.181
  61.7 0.5 pad_maximum_fusion.7
  62.2 0.3 slice_subtract_fusion
  62.6 0.7 minimum_multiply_fusion
  63.3 0.7 fusion.4
  64.1 0.2 multiply_bitcast_fusion
  65.1 0.5 subtract_multiply_fusion
  66.1 1.9 %collective-permute-start.6 = (f32[8,2,20,128]{3,0,2,1:T(8,128)S(1)}, f32[8,2,20,128]{3,0,2,1:T(8,128)S(1)}, u32[]{:S(2)}, u32[]{:S(2)}) collective-permute-start(f32[8,2,20,128]{3,0,2,1:T(8,128)S(1)} %copy.702), channel_id=1, source_target_pairs={{0,4},{4,8},{8,12},{12,16},{16,20},{20,24},{24,28},{28,32},{32,36}... | collective-permute-start | bytes 491528 | tf_op jit(solution)/shard_map/ppermute | solution.py:55
  68.1 6.0 %collective-permute-start.7 = (f32[8,2,20,128]{3,0,2,1:T(8,128)S(1)}, f32[8,2,20,128]{3,0,2,1:T(8,128)S(1)}, u32[]{:S(2)}, u32[]{:S(2)}) collective-permute-start(f32[8,2,20,128]{3,0,2,1:T(8,128)S(1)} %copy.706), channel_id=1, source_target_pairs={{4,0},{8,4},{12,8},{16,12},{20,16},{24,20},{28,24},{32,28},{36,32}... | collective-permute-start | bytes 491528 | tf_op jit(solution)/shard_map/ppermute | solution.py:56
  74.1 0.6 minimum_multiply_fusion.2
  74.7 0.3 fusion.8
  75.0 0.2 multiply_bitcast_fusion.2
  75.5 0.2 multiply_subtract_fusion
  75.9 0.8 %collective-permute-done.7 = f32[8,2,20,128]{3,0,2,1:T(8,128)S(1)} collective-permute-done((f32[8,2,20,128]{3,0,2,1:T(8,128)S(1)}, f32[8,2,20,128]{3,0,2,1:T(8,128)S(1)}, u32[]{:S(2)}, u32[]{:S(2)}) %collective-permute-start.7) | collective-permute-done | bytes 163872 | tf_op jit(solution)/shard_map/ppermute | solution.py:56
  76.7 0.1 pad_maximum_fusion.1
  77.0 0.3 minimum_multiply_fusion.4
  77.3 0.1 fusion.12
  77.4 0.1 multiply_bitcast_fusion.4
  77.9 0.2 subtract_multiply_fusion.2
  78.1 1.2 %fusion.32 = f32[8,8,16,128]{3,2,1,0:T(8,128)} fusion(f32[8,8,16,128]{3,2,1,0:T(8,128)S(1)} %copy-done, f32[8,8,16,128]{3,2,1,0:T(8,128)S(1)} %fusion.28, f32[8,8,16,128]{3,2,1,0:T(8,128)S(1)} %constant_dynamic-update-slice_fusion.55, f32[8,8,17,128]{3,2,1,0:T(8,128)S(1)} %multiply_subtract_fusion, f32[8,8,16,129]{3,2,1,0:T(8,128)S(1)} %subtract_multiply_fusion, ...), kind=kLoop, calls=%fused_computation.97 | loop fusion | flops 1703936 | bytes 5251104 | tf_op jit(solution)/shard_map/add | solution.py:228
  (166 shorter events, 5.2 us)
Async XLA Ops:
  0.6 9.4 %copy-start = (f32[8,8,16,128]{3,2,1,0:T(8,128)S(1)}, f32[8,8,16,128]{3,2,1,0:T(8,128)}, u32[]{:S(2)}) copy-start(f32[8,8,16,128]{3,2,1,0:T(8,128)} %param.2) | copy-start | bytes 1572868
  1.8 41.8 %collective-permute-start = (f32[8,8,2,128]{3,1,2,0:T(8,128)S(1)}, f32[8,8,2,128]{3,1,2,0:T(8,128)S(1)}, u32[]{:S(2)}, u32[]{:S(2)}) collective-permute-start(f32[8,8,2,128]{3,1,2,0:T(8,128)S(1)} %copy.721), channel_id=1, source_target_pairs={{0,1},{1,2},{2,3},{3,0},{4,5},{5,6},{6,7},{7,4},{8,9},{9,10},{10,1... | collective-permute-start | bytes 196616 | tf_op jit(solution)/shard_map/ppermute | solution.py:55
  3.5 40.2 %collective-permute-start.1 = (f32[8,8,2,128]{3,1,2,0:T(8,128)S(1)}, f32[8,8,2,128]{3,1,2,0:T(8,128)S(1)}, u32[]{:S(2)}, u32[]{:S(2)}) collective-permute-start(f32[8,8,2,128]{3,1,2,0:T(8,128)S(1)} %copy.722), channel_id=1, source_target_pairs={{1,0},{2,1},{3,2},{0,3},{5,4},{6,5},{7,6},{4,7},{9,8},{10,9},{11,1... | collective-permute-start | bytes 196616 | tf_op jit(solution)/shard_map/ppermute | solution.py:56
  6.7 9.9 %all-to-all-start = ((f32[4,1,8]{2,1,0:T(1,128)}), f32[4,1,8]{2,1,0:T(1,128)S(1)}, u32[]{:S(2)}, u32[]{:S(2)}) async-start(f32[4,1,8]{2,1,0:T(1,128)} %broadcast_in_dim.45), calls=%async_computation | async-start | bytes 4096 | tf_op jit(solution)/shard_map/all_to_all | solution.py:19
  18.6 20.6 %all-to-all-start.1 = ((f32[64,1,1]{2,1,0:T(1,128)}), f32[64,1,1]{2,1,0:T(1,128)S(1)}, u32[]{:S(2)}, u32[]{:S(2)}) async-start(f32[64,1,1]{2,1,0:T(1,128)} %broadcast_in_dim.46), calls=%async_computation.1 | async-start | bytes 65536 | tf_op jit(solution)/shard_map/all_to_all | solution.py:19
  44.0 6.6 %collective-permute-start.3 = (f32[8,2,20,128]{3,0,2,1:T(8,128)S(1)}, f32[8,2,20,128]{3,0,2,1:T(8,128)S(1)}, u32[]{:S(2)}, u32[]{:S(2)}) collective-permute-start(f32[8,2,20,128]{3,0,2,1:T(8,128)S(1)} %copy.686), channel_id=1, source_target_pairs={{4,0},{8,4},{12,8},{16,12},{20,16},{24,20},{28,24},{32,28},{36,32}... | collective-permute-start | bytes 491528 | tf_op jit(solution)/shard_map/ppermute | solution.py:56
  46.9 8.7 %collective-permute-start.2 = (f32[8,2,20,128]{3,0,2,1:T(8,128)S(1)}, f32[8,2,20,128]{3,0,2,1:T(8,128)S(1)}, u32[]{:S(2)}, u32[]{:S(2)}) collective-permute-start(f32[8,2,20,128]{3,0,2,1:T(8,128)S(1)} %copy.682), channel_id=1, source_target_pairs={{0,4},{4,8},{8,12},{12,16},{16,20},{20,24},{24,28},{28,32},{32,36}... | collective-permute-start | bytes 491528 | tf_op jit(solution)/shard_map/ppermute | solution.py:55
  57.9 7.8 %collective-permute-start.4 = (f32[8,8,2,128]{3,1,2,0:T(8,128)S(1)}, f32[8,8,2,128]{3,1,2,0:T(8,128)S(1)}, u32[]{:S(2)}, u32[]{:S(2)}) collective-permute-start(f32[8,8,2,128]{3,1,2,0:T(8,128)S(1)} %copy.696), channel_id=1, source_target_pairs={{0,1},{1,2},{2,3},{3,0},{4,5},{5,6},{6,7},{7,4},{8,9},{9,10},{10,1... | collective-permute-start | bytes 196616 | tf_op jit(solution)/shard_map/ppermute | solution.py:55
  60.0 5.7 %collective-permute-start.5 = (f32[8,8,2,128]{3,1,2,0:T(8,128)S(1)}, f32[8,8,2,128]{3,1,2,0:T(8,128)S(1)}, u32[]{:S(2)}, u32[]{:S(2)}) collective-permute-start(f32[8,8,2,128]{3,1,2,0:T(8,128)S(1)} %copy.697), channel_id=1, source_target_pairs={{1,0},{2,1},{3,2},{0,3},{5,4},{6,5},{7,6},{4,7},{9,8},{10,9},{11,1... | collective-permute-start | bytes 196616 | tf_op jit(solution)/shard_map/ppermute | solution.py:56
  66.1 9.7 %collective-permute-start.6 = (f32[8,2,20,128]{3,0,2,1:T(8,128)S(1)}, f32[8,2,20,128]{3,0,2,1:T(8,128)S(1)}, u32[]{:S(2)}, u32[]{:S(2)}) collective-permute-start(f32[8,2,20,128]{3,0,2,1:T(8,128)S(1)} %copy.702), channel_id=1, source_target_pairs={{0,4},{4,8},{8,12},{12,16},{16,20},{20,24},{24,28},{28,32},{32,36}... | collective-permute-start | bytes 491528 | tf_op jit(solution)/shard_map/ppermute | solution.py:55
  68.1 8.6 %collective-permute-start.7 = (f32[8,2,20,128]{3,0,2,1:T(8,128)S(1)}, f32[8,2,20,128]{3,0,2,1:T(8,128)S(1)}, u32[]{:S(2)}, u32[]{:S(2)}) collective-permute-start(f32[8,2,20,128]{3,0,2,1:T(8,128)S(1)} %copy.706), channel_id=1, source_target_pairs={{4,0},{8,4},{12,8},{16,12},{20,16},{24,20},{28,24},{32,28},{36,32}... | collective-permute-start | bytes 491528 | tf_op jit(solution)/shard_map/ppermute | solution.py:56
where the time goes:
time: 79.7 us; the launch traced here: 79.3 us
  starting transfers between devices  34.8 us (44%)
  other arithmetic  18.4 us (23%)
  waiting for transfers between devices  13.5 us (17%)
  local copies, waits for them, and re-layouts  8.12 us (10%)
  between operations  4.41 us (6%)
    all_to_all x2, starting transfers between devices, from_everyone(): lax.all_to_all(jnp.broadcast_to(value[None], (peers, *value.shape)), axis...  15.3 us
    ppermute x4, starting transfers between devices, extended_2(): after = lax.ppermute(initial, axis, down)  11.7 us
    ppermute x4, starting transfers between devices, extended_2(): before = lax.ppermute(last, axis, up)  7.77 us
    all_to_all x2, waiting for transfers between devices, from_everyone(): lax.all_to_all(jnp.broadcast_to(value[None], (peers, *value.shape)), axis...  7.71 us
    ppermute x4, waiting for transfers between devices, extended_2(): before = lax.ppermute(last, axis, up)  4.95 us
    mul x6, other arithmetic, face_flux(): 0.5 * (jnp.sign(below_diff) + jnp.sign(above_diff))  3.14 us
    unnamed x93, other arithmetic  3.07 us
    add x6, other arithmetic, face_flux(): lax.slice_in_dim(values, 1, interior + 2, axis=along_dim)  2.36 us
  transfers between devices with their start and end apart: 10, of which 3 were waited for; matrix products, arithmetic and copies ran while one was open for 25% of the time, Pallas kernels for 0%

commit v1 on v0

v1 whole, which is shorter than its diff:
```python
import functools
import math

import jax
import jax.numpy as jnp
import numpy as np
from jax import lax
from jax.experimental import pallas as pl
from jax.experimental.pallas import tpu as pltpu
from jax.sharding import PartitionSpec as P

ADIABATIC = 4.0 / 3.0
INNER_RADIUS = 1.0
OUTER_RADIUS = 2.0
COURANT = 0.4
GRAVITY_KICK = 0.004
MINIMUM_DENSITY = 0.05
PRESSURE_FLOOR = 0.01

NV = 8
MESH = pl.DeviceIdType.MESH


def step_sizes(radial_total, phi_total, theta_total):
    theta_step = math.pi / theta_total
    phi_step = 2.0 * math.pi / phi_total
    polar_width = INNER_RADIUS * math.sin(0.5 * theta_step) * phi_step
    radial_step = min(2.0 * polar_width, (OUTER_RADIUS - INNER_RADIUS) / radial_total)
    timestep = COURANT * min(radial_step, polar_width)
    return (radial_step, theta_step, phi_step, timestep)


def half_slope(low, high):
    return jnp.maximum(jnp.minimum(low, high), jnp.minimum(jnp.maximum(low, high), 0.0))


def face_side(state, component):
    density = jnp.maximum(state[0], MINIMUM_DENSITY)
    inverse = 1.0 / density
    squares = state[1] * state[1] + state[2] * state[2] + state[3] * state[3]
    pressure = jnp.maximum(
        (ADIABATIC - 1.0) * (state[4] - 0.5 * squares * inverse), PRESSURE_FLOOR * density
    )
    normal = state[component] * inverse
    square = ADIABATIC * pressure * inverse
    sound = square * lax.rsqrt(square)
    return pressure, normal, jnp.abs(normal) + sound


def twice_flux(left, right, component):
    left_p, left_v, left_s = face_side(left, component)
    right_p, right_v, right_s = face_side(right, component)
    signal = jnp.maximum(left_s, right_s)
    left_w, right_w = left_v + signal, right_v - signal
    flux = [left[k] * left_w + right[k] * right_w for k in range(NV)]
    flux[component] = flux[component] + (left_p + right_p)
    flux[4] = flux[4] + (left_p * left_v + right_p * right_v)
    return flux


def edge_pair(cells, component):
    lefts, rights = [], []
    for k in range(NV):
        halves = [0.5 * (cells[i + 1][k] - cells[i][k]) for i in range(4)]
        slopes = [half_slope(halves[i], halves[i + 1]) for i in range(3)]
        lefts.append((cells[1][k] + slopes[0], cells[2][k] + slopes[1]))
        rights.append((cells[2][k] - slopes[1], cells[3][k] - slopes[2]))
    return [
        twice_flux([a[i] for a in lefts], [b[i] for b in rights], component) for i in range(2)
    ]


def kernel(
    sizes, state_hbm, mass_smem, angles_hbm,
    out_hbm, enclosed_ref,
    u0, u1, hr0, hr1, hp0, hp1, pk0, pk1, sr, acc, fp, fr, sl, outv,
    m1, m2, tab, grav, ct,
    in_sem, out_sem, halo_send, halo_recv, m1_send, m1_recv, m2_send, m2_recv,
):
    rows, width, slabs, wedges, groups, radial_step, theta_step, phi_step, timestep = sizes
    strength = GRAVITY_KICK / timestep
    place = lax.axis_index("radial")
    wedge = lax.axis_index("phi")
    inner = slabs // groups
    group, member = place // inner, lax.rem(place, inner)
    span = width + 8

    def at(radial, phi):
        return {"radial": radial, "phi": phi}

    up, down = lax.rem(place + 1, slabs), lax.rem(place + slabs - 1, slabs)
    east, west = lax.rem(wedge + 1, wedges), lax.rem(wedge + wedges - 1, wedges)
    plane = [
        at(lax.rem(place + inner * (j // wedges), slabs), lax.rem(wedge + j % wedges, wedges))
        for j in range(groups * wedges)
    ]
    column = [at(group * inner + lax.rem(member + j, inner), wedge) for j in range(inner)]

    fetch = pltpu.make_async_copy(state_hbm, u0.at[:, pl.ds(8, rows * width), :], in_sem.at[0])
    fetch.start()
    fetch_angles = pltpu.make_async_copy(angles_hbm, ct, in_sem.at[1])
    fetch_angles.start()

    barrier = pltpu.get_barrier_semaphore()
    greeted = plane[1:] + column[1:] + [at(up, wedge), at(down, wedge)]
    for peer in greeted:
        pl.semaphore_signal(barrier, inc=1, device_id=peer, device_id_type=MESH)

    row = lax.broadcasted_iota(jnp.int32, (8, 128), 0)
    lane = lax.broadcasted_iota(jnp.int32, (8, 128), 1)
    first = place * rows

    def radius_of(index):
        return INNER_RADIUS + (index.astype(jnp.float32) + 0.5) * radial_step

    radius = radius_of(first + row)
    inverse_radius = 1.0 / radius
    low_face, high_face = radius - 0.5 * radial_step, radius + 0.5 * radial_step
    area = inverse_radius * inverse_radius * (0.5 * timestep / radial_step)
    tab[0] = timestep * inverse_radius
    tab[1] = low_face * low_face * area
    tab[2] = high_face * high_face * area

    fetch_angles.wait()
    fetch.wait()

    total = u0[0, pl.ds(8, 8, stride=width), :]
    for f in range(1, width):
        total = total + u0[0, pl.ds(8 + f, 8, stride=width), :]
    shells = jnp.sum(total * ct[3:4, :], axis=1, keepdims=True) * (
        radius * radius * (radial_step * theta_step * phi_step)
    )
    m1[0] = jnp.sum(jnp.where(lane == member * rows + row, shells, 0.0), axis=0, keepdims=True)

    def pack(source, packed):
        for side, zones in enumerate(((width - 2, width - 1), (0, 1))):
            for k in range(NV):
                for i, zone in enumerate(zones):
                    packed[side, k, i] = source[k, pl.ds(8 + zone, 8, stride=width), :]

    pack(u0, pk0)
    pl.semaphore_wait(barrier, len(greeted))

    m1_copies = [
        pltpu.make_async_remote_copy(
            src_ref=m1.at[0], dst_ref=m1.at[j], send_sem=m1_send.at[j], recv_sem=m1_recv.at[j],
            device_id=plane[j], device_id_type=MESH,
        )
        for j in range(1, groups * wedges)
    ]
    for copy in m1_copies:
        copy.start()

    def halo_copies(number, high_rows, low_rows, packed, radial_halo, phi_halo):
        def copy(which, source, target, peer):
            return pltpu.make_async_remote_copy(
                src_ref=source, dst_ref=target, send_sem=halo_send.at[4 * number + which],
                recv_sem=halo_recv.at[4 * number + which], device_id=peer, device_id_type=MESH,
            )

        return (
            copy(0, high_rows, radial_halo.at[0], at(up, wedge)),
            copy(1, low_rows, radial_halo.at[1], at(down, wedge)),
            copy(2, packed.at[0], phi_halo.at[0], at(place, east)),
            copy(3, packed.at[1], phi_halo.at[1], at(place, west)),
        )

    def start_halos(copies, radial_halo, low_row, high_row):
        pl.when(place < slabs - 1)(lambda: copies[0].start())
        pl.when(place > 0)(lambda: copies[1].start())
        copies[2].start()
        copies[3].start()

        @pl.when(place == 0)
        def _():
            for k in range(NV):
                for i in range(2):
                    radial_halo[0, k, pl.ds(width * i, width), :] = low_row(k)

        @pl.when(place == slabs - 1)
        def _():
            for k in range(NV):
                for i in range(2):
                    radial_halo[1, k, pl.ds(width * i, width), :] = high_row(k)

    def wait_radial(copies):
        pl.when(place > 0)(lambda: copies[0].wait_recv())
        pl.when(place < slabs - 1)(lambda: copies[1].wait_recv())

    def wait_sent(copies):
        pl.when(place < slabs - 1)(lambda: copies[0].wait_send())
        pl.when(place > 0)(lambda: copies[1].wait_send())
        copies[2].wait_send()
        copies[3].wait_send()

    first_halos = halo_copies(
        0, u0.at[:, pl.ds(8 + (rows - 2) * width, 2 * width), :], u0.at[:, pl.ds(8, 2 * width), :],
        pk0, hr0, hp0,
    )
    start_halos(
        first_halos, hr0,
        lambda k: u0[k, pl.ds(8, width), :],
        lambda k: u0[k, pl.ds(8 + (rows - 1) * width, width), :],
    )

    wide_lane = lax.broadcasted_iota(jnp.int32, (width, 128), 1)

    def polar_and_azimuth(u):
        def one_row(r, carry):
            base = pl.multiple_of(8 + r * width, 8)
            here = pl.ds(base, width)
            cells = [u[k, here, :] for k in range(NV)]
            scale = tab[0, pl.ds(r, 1), :]
            density = jnp.maximum(cells[0], MINIMUM_DENSITY)
            inverse = 1.0 / density
            speed = [None] + [cells[m] * inverse for m in (1, 2, 3)]
            squares = cells[1] * speed[1] + cells[2] * speed[2] + cells[3] * speed[3]
            pressure = jnp.maximum(
                (ADIABATIC - 1.0) * (cells[4] - 0.5 * squares), PRESSURE_FLOOR * density
            )
            cotangent = ct[2:3, :]
            spin = cells[3] * speed[3]
            source = [None] * NV
            source[1] = 2.0 * pressure + (cells[2] * speed[2] + spin)
            source[2] = (pressure + spin) * cotangent - cells[1] * speed[2]
            source[3] = -speed[3] * (cells[1] + cells[2] * cotangent)
            mask = ct[4:5, :]
            left, right = [], []
            for k in range(NV):
                high = (pltpu.roll(cells[k], 127, 1) - cells[k]) * mask
                slope = half_slope(pltpu.roll(high, 1, 1), high)
                left.append(cells[k] + slope)
                right.append(
                    jnp.where(wide_lane == 127, cells[k], pltpu.roll(cells[k] - slope, 127, 1))
                )
            flux = twice_flux(left, right, 2)
            sine, inverse_sine = ct[0:1, :], ct[1:2, :]
            for k in range(NV):
                through = flux[k] * sine
                change = (pltpu.roll(through, 1, 1) - through) * inverse_sine
                if source[k] is not None:
                    change = change + source[k]
                acc[k, pl.ds(pl.multiple_of(r * width, 8), width), :] = cells[k] + scale * change
            left, right = [], []
            for k in range(NV):
                low = 0.5 * (cells[k] - u[k, pl.ds(base - 1, width), :])
                high = 0.5 * (u[k, pl.ds(base + 1, width), :] - cells[k])
                slope = half_slope(low, high)
                left.append(pltpu.roll(cells[k] + slope, 1, 0))
                right.append(cells[k] - slope)
            flux = twice_flux(left, right, 3)
            for k in range(NV):
                fp[k, pl.ds(pl.multiple_of(r * span, 8), width), :] = flux[k]
            return carry

        lax.fori_loop(0, rows, one_row, 0)

    def inner_radial(u):
        def one_row(r, carry):
            base = pl.multiple_of(8 + r * width, 8)
            store = pl.multiple_of(r * width, 8)
            right = []
            left = []
            for k in range(NV):
                cell = u[k, pl.ds(base, width), :]
                low = 0.5 * (cell - u[k, pl.ds(base - width, width), :])
                high = 0.5 * (u[k, pl.ds(base + width, width), :] - cell)
                slope = half_slope(low, high)
                right.append(cell - slope)
                left.append(sl[k, pl.ds(store - width, width), :])
                sl[k, pl.ds(store, width), :] = cell + slope
            flux = twice_flux(left, right, 1)
            for k in range(NV):
                fr[k, pl.ds(store, width), :] = flux[k]
            return carry

        lax.fori_loop(1, rows - 1, one_row, 0)

    def edge_azimuth(u, halo):
        for side in range(2):
            own = (0, 1, 2) if side == 0 else (width - 3, width - 2, width - 1)
            inside = [
                [u[k, pl.ds(8 + f, 8, stride=width), :] for k in range(NV)] for f in own
            ]
            outside = [[halo[side, k, i] for k in range(NV)] for i in range(2)]
            cells = outside + inside if side == 0 else inside + outside
            fluxes = edge_pair(cells, 3)
            faces = (0, 1) if side == 0 else (width - 1, width)
            for face, flux in zip(faces, fluxes):
                for k in range(NV):
                    fp[k, pl.ds(face, 8, stride=span), :] = flux[k]

    def edge_radial(u, halo):
        for side in range(2):
            own = (0, 1, 2) if side == 0 else (rows - 3, rows - 2, rows - 1)
            inside = [[u[k, pl.ds(8 + r * width, width), :] for k in range(NV)] for r in own]
            outside = [
                [halo[side, k, pl.ds(width * i, width), :] for k in range(NV)] for i in range(2)
            ]
            cells = outside + inside if side == 0 else inside + outside
            fluxes = edge_pair(cells, 1)
            faces = (0, 1) if side == 0 else (rows - 1, rows)
            for face, flux in zip(faces, fluxes):
                for k in range(NV):
                    fr[k, pl.ds(face * width, width), :] = flux[k]

    azimuth_scale = 0.5 / phi_step

    def advanced_row(r):
        store = pl.multiple_of(r * width, 8)
        low_area, high_area = tab[1, pl.ds(r, 1), :], tab[2, pl.ds(r, 1), :]
        across = tab[0, pl.ds(r, 1), :] * ct[1:2, :] * azimuth_scale
        below = pl.multiple_of(r * span, 8)
        values = []
        for k in range(NV):
            values.append(
                acc[k, pl.ds(store, width), :]
                + across * (fp[k, pl.ds(below, width), :] - fp[k, pl.ds(below + 1, width), :])
                + low_area * fr[k, pl.ds(store, width), :]
                - high_area * fr[k, pl.ds(pl.multiple_of(store + width, 8), width), :]
            )
        return values

    polar_and_azimuth(u0)
    inner_radial(u0)

    for copy in m1_copies:
        copy.wait_recv()
    for i in range(groups):
        shell = m1[i * wedges]
        for j in range(1, wedges):
            shell = shell + m1[i * wedges + j]
        m2[0, i : i + 1, :] = shell
    m2_copies = [
        pltpu.make_async_remote_copy(
            src_ref=m2.at[0], dst_ref=m2.at[j], send_sem=m2_send.at[j], recv_sem=m2_recv.at[j],
            device_id=column[j], device_id_type=MESH,
        )
        for j in range(1, inner)
    ]
    for copy in m2_copies:
        copy.start()

    first_halos[2].wait_recv()
    first_halos[3].wait_recv()
    edge_azimuth(u0, hp0)
    wait_radial(first_halos)
    edge_radial(u0, hr0)

    def section_one_row(r, carry):
        values = advanced_row(r)
        for k in range(NV):
            u1[k, pl.ds(pl.multiple_of(8 + r * width, 8), width), :] = values[k]
        return carry

    lax.fori_loop(0, rows, section_one_row, 0)
    pack(u1, pk1)
    for k in range(NV):
        sr[0, k] = u1[k, pl.ds(8 + (rows - 2) * width, 2 * width), :]
        sr[1, k] = u1[k, pl.ds(8, 2 * width), :]
    second_halos = halo_copies(1, sr.at[0], sr.at[1], pk1, hr1, hp1)
    start_halos(
        second_halos, hr1,
        lambda k: sr[1, k, pl.ds(0, width), :],
        lambda k: sr[0, k, pl.ds(width, width), :],
    )

    for copy in m2_copies:
        copy.wait_recv()
    table = m2[0]
    for j in range(1, inner):
        table = table + m2[j]
    last = slabs * rows - 1
    beyond = jnp.clip(first + jnp.where(row < 2, row - 2, rows - 2 + row), 0, last)
    enclosed = []
    for target in (first + row, beyond):
        inside = jnp.zeros((8, 128), jnp.float32)
        for i in range(groups):
            index = lax.rem(group + groups - i, groups) * (inner * rows) + lane
            share = jnp.where(index < target, 1.0, jnp.where(index == target, 0.5, 0.0))
            inside = inside + share * table[i : i + 1, :]
        enclosed.append(jnp.sum(inside, axis=1, keepdims=True) + mass_smem[0])
    for i, target in enumerate((first + row, beyond)):
        inverse = 1.0 / radius_of(target)
        grav[8 * i : 8 * i + 8, :] = (timestep * strength) * enclosed[i] * inverse * inverse
    enclosed_ref[...] = jnp.sum(
        jnp.where(lane == row, enclosed[0], 0.0), axis=0, keepdims=True
    )[:, :rows]

    def gravity_row(r, carry):
        base = pl.ds(pl.multiple_of(8 + r * width, 8), width)
        pull = grav[pl.ds(r, 1), :]
        u1[1, base, :] = u1[1, base, :] - pull * jnp.maximum(u0[0, base, :], MINIMUM_DENSITY)
        u1[4, base, :] = u1[4, base, :] - pull * u0[1, base, :]
        return carry

    lax.fori_loop(0, rows, gravity_row, 0)

    polar_and_azimuth(u1)
    inner_radial(u1)
    second_halos[2].wait_recv()
    second_halos[3].wait_recv()
    pull = grav[0:8, :]
    for side in range(2):
        for i in range(2):
            hp1[side, 1, i] = hp1[side, 1, i] - pull * jnp.maximum(
                hp0[side, 0, i], MINIMUM_DENSITY
            )
            hp1[side, 4, i] = hp1[side, 4, i] - pull * hp0[side, 1, i]
    edge_azimuth(u1, hp1)
    wait_radial(second_halos)
    for side in range(2):
        for i in range(2):
            which = pl.ds(width * i, width)
            pull = grav[8 + 2 * side + i : 9 + 2 * side + i, :]
            hr1[side, 1, which, :] = hr1[side, 1, which, :] - pull * jnp.maximum(
                hr0[side, 0, which, :], MINIMUM_DENSITY
            )
            hr1[side, 4, which, :] = hr1[side, 4, which, :] - pull * hr0[side, 1, which, :]
    edge_radial(u1, hr1)

    def section_two_row(r, carry):
        values = advanced_row(r)
        base = pl.ds(pl.multiple_of(8 + r * width, 8), width)
        pull = grav[pl.ds(r, 1), :]
        values[1] = values[1] - pull * jnp.maximum(u1[0, base, :], MINIMUM_DENSITY)
        values[4] = values[4] - pull * u1[1, base, :]
        for k in range(NV):
            outv[k, pl.ds(pl.multiple_of(r * width, 8), width), :] = 0.5 * (
                u0[k, base, :] + values[k]
            )
        return carry

    lax.fori_loop(0, rows, section_two_row, 0)
    give = pltpu.make_async_copy(outv, out_hbm, out_sem.at[0])
    give.start()
    for copy in m1_copies + m2_copies:
        copy.wait_send()
    wait_sent(first_halos)
    wait_sent(second_halos)
    give.wait()


def body(groups, conserved, core_mass):
    _, rows, width, lanes = conserved.shape
    slabs, wedges = lax.axis_size("radial"), lax.axis_size("phi")
    inner = slabs // groups
    radial_step, theta_step, phi_step, timestep = step_sizes(rows * slabs, width * wedges, lanes)
    centers = (np.arange(lanes) + 0.5) * theta_step
    faces = (np.arange(lanes) + 1.0) * theta_step
    angles = np.zeros((8, lanes))
    angles[0] = np.sin(faces) * (0.5 / theta_step)
    angles[1] = 1.0 / np.sin(centers)
    angles[2] = np.cos(centers) / np.sin(centers)
    angles[3] = np.sin(centers)
    angles[4] = np.where(np.arange(lanes) == lanes - 1, 0.0, 0.5)
    angles = jnp.asarray(angles.astype(np.float32))
    sizes = (rows, width, slabs, wedges, groups, radial_step, theta_step, phi_step, timestep)
    f32 = jnp.float32
    vmem = lambda *shape: pltpu.VMEM(shape, f32)
    dma = lambda count: pltpu.SemaphoreType.DMA((count,))
    cells = rows * width
    advanced, enclosed = pl.pallas_call(
        functools.partial(kernel, sizes),
        out_shape=(
            jax.ShapeDtypeStruct((NV, cells, lanes), f32),
            jax.ShapeDtypeStruct((1, rows), f32),
        ),
        in_specs=[
            pl.BlockSpec(memory_space=pl.ANY),
            pl.BlockSpec(memory_space=pltpu.SMEM),
            pl.BlockSpec(memory_space=pl.ANY),
        ],
        out_specs=(
            pl.BlockSpec(memory_space=pl.ANY),
            pl.BlockSpec(memory_space=pltpu.VMEM),
        ),
        scratch_shapes=[
            vmem(NV, cells + 16, lanes), vmem(NV, cells + 16, lanes),
            vmem(2, NV, 2 * width, lanes), vmem(2, NV, 2 * width, lanes),
            vmem(2, NV, 2, 8, lanes), vmem(2, NV, 2, 8, lanes),
            vmem(2, NV, 2, 8, lanes), vmem(2, NV, 2, 8, lanes),
            vmem(2, NV, 2 * width, lanes),
            vmem(NV, cells, lanes),
            vmem(NV, rows * (width + 8), lanes),
            vmem(NV, cells + width, lanes),
            vmem(NV, cells, lanes),
            vmem(NV, cells, lanes),
            vmem(groups * wedges, 1, lanes), vmem(inner, groups, lanes),
            vmem(3, 8, lanes), vmem(16, lanes), vmem(8, lanes),
            dma(2), dma(1), dma(8), dma(8),
            dma(groups * wedges), dma(groups * wedges), dma(inner), dma(inner),
        ],
        compiler_params=pltpu.CompilerParams(collective_id=0, has_side_effects=True),
    )(conserved.reshape(NV, cells, lanes), core_mass, angles)
    return advanced.reshape(conserved.shape), enclosed.reshape(rows)


def solution(mesh):
    in_specs = (P(None, "radial", "phi", None), P())
    out_specs = (P(None, "radial", "phi", None), P("radial"))
    return jax.shard_map(
        functools.partial(body, 4), mesh=mesh, in_specs=in_specs, out_specs=out_specs,
        check_vma=False,
    )
```

time: 79.7 us -> 29.4 us (0.37)
  the two profiles are of different devices: /device:TPU:2 before, /device:TPU:1 now
where the time goes in v1:
time: 29.4 us; the launch traced here: 29.3 us
  Pallas kernels  25.6 us (87%)
  local copies, waits for them, and re-layouts  2.38 us (8%)
  between operations  1.29 us (4%)
    pallas_call x1, Pallas kernels, body(): pl.pallas_call(functools.partial(kernel, sizes), out_shape=(jax.ShapeDtyp...  25.6 us
    unnamed x4, local copies, waits for them, and re-layouts  2.38 us

profile of v1, /device:TPU:1, one launch (start us, length us, event | category | flops | bytes accessed | tf_op | source)
XLA Modules:
  0.0 29.3 jit_solution(18371572085563642259)
XLA Ops:
  1.3 25.6 %shard_map.50 = (f32[8,128,128]{2,1,0:T(8,128)}, f32[1,8]{1,0:T(1,128)}) custom-call(f32[8,128,128]{2,1,0:T(8,128)} %bitcast.3, f32[1]{0:T(128)S(6)} %copy.7.mass_smem, f32[8,128]{1,0:T(8,128)} %constant.2.clone.angles_hbm), custom_call_target="tpu_custom_call" | custom-call | tf_op jit(solution)/shard_map/pallas_call | solution.py:463
  26.9 0.0 copy-start
  26.9 1.9 %copy.8 = f32[8,8,16,128]{3,2,1,0:T(8,128)} copy(f32[8,8,16,128]{3,2,1,0:T(8,128)} %bitcast.4) | data formatting | bytes 1048576
  28.8 0.0 copy-done
  28.8 0.5 %copy.9 = f32[8]{0:T(128)} copy(f32[8]{0:T(128)S(1)} %bitcast.5) | data formatting | bytes 64
Async XLA Ops:
  26.9 1.9 %copy-start = (f32[1,8]{1,0:T(1,128)S(1)}, f32[1,8]{1,0:T(1,128)}, u32[]{:S(2)}) copy-start(f32[1,8]{1,0:T(1,128)} %get-tuple-element.5) | copy-start | bytes 100

commit v2 on v1

--- a/solution.py
+++ b/solution.py
@@ -70,41 +70,86 @@
     ]
 
 
+def sources(cells, cotangent):
+    density = jnp.maximum(cells[0], MINIMUM_DENSITY)
+    inverse = 1.0 / density
+    speed = [None] + [cells[m] * inverse for m in (1, 2, 3)]
+    squares = cells[1] * speed[1] + cells[2] * speed[2] + cells[3] * speed[3]
+    pressure = jnp.maximum(
+        (ADIABATIC - 1.0) * (cells[4] - 0.5 * squares), PRESSURE_FLOOR * density
+    )
+    spin = cells[3] * speed[3]
+    source = [None] * NV
+    source[1] = 2.0 * pressure + (cells[2] * speed[2] + spin)
+    source[2] = (pressure + spin) * cotangent - cells[1] * speed[2]
+    source[3] = -speed[3] * (cells[1] + cells[2] * cotangent)
+    return source
+
+
 def kernel(
-    sizes, state_hbm, mass_smem, angles_hbm,
-    out_hbm, enclosed_ref,
-    u0, u1, hr0, hr1, hp0, hp1, pk0, pk1, sr, acc, fp, fr, sl, outv,
-    m1, m2, tab, grav, ct,
-    in_sem, out_sem, halo_send, halo_recv, m1_send, m1_recv, m2_send, m2_recv,
+    sizes, state_hbm, mass_hbm, angles_hbm,
+    outv, enclosed_ref,
+    u0, u1, hr0, hr1, hp0, hp1, pk0, pk1, sr, acc, fp, fr, sl, lt, rt, th,
+    shared, below_above, wedge_rows, tab, grav, ct, core,
+    in_sem, halo_send, halo_recv, shared_send, shared_recv, side_send, side_recv,
+    wedge_send, wedge_recv, from_higher, from_opposite,
 ):
     rows, width, slabs, wedges, groups, radial_step, theta_step, phi_step, timestep = sizes
     strength = GRAVITY_KICK / timestep
     place = lax.axis_index("radial")
     wedge = lax.axis_index("phi")
     inner = slabs // groups
+    levels = inner // 2
     group, member = place // inner, lax.rem(place, inner)
+    level, core_index = member // 2, lax.rem(member, 2)
     span = width + 8
+    last = slabs - 1
 
     def at(radial, phi):
         return {"radial": radial, "phi": phi}
 
-    up, down = lax.rem(place + 1, slabs), lax.rem(place + slabs - 1, slabs)
+    def signal(semaphore, radial, phi):
+        pl.semaphore_signal(semaphore, inc=1, device_id=at(radial, phi), device_id_type=MESH)
+
     east, west = lax.rem(wedge + 1, wedges), lax.rem(wedge + wedges - 1, wedges)
-    plane = [
-        at(lax.rem(place + inner * (j // wedges), slabs), lax.rem(wedge + j % wedges, wedges))
-        for j in range(groups * wedges)
-    ]
-    column = [at(group * inner + lax.rem(member + j, inner), wedge) for j in range(inner)]
-
-    fetch = pltpu.make_async_copy(state_hbm, u0.at[:, pl.ds(8, rows * width), :], in_sem.at[0])
-    fetch.start()
-    fetch_angles = pltpu.make_async_copy(angles_hbm, ct, in_sem.at[1])
-    fetch_angles.start()
+    opposite = lax.rem(wedge + wedges // 2, wedges)
+
+    fetch_mass = pltpu.make_async_copy(mass_hbm, core, in_sem.at[3])
+    fetch_density = pltpu.make_async_copy(
+        state_hbm.at[pl.ds(0, 1)], u0.at[pl.ds(0, 1), pl.ds(8, rows * width), :], in_sem.at[0]
+    )
+    fetch = pltpu.make_async_copy(
+        state_hbm.at[pl.ds(1, NV - 1)], u0.at[pl.ds(1, NV - 1), pl.ds(8, rows * width), :],
+        in_sem.at[1],
+    )
+    fetch_angles = pltpu.make_async_copy(angles_hbm, ct, in_sem.at[2])
+    for copy in (fetch_density, fetch_angles, fetch, fetch_mass):
+        copy.start()
 
     barrier = pltpu.get_barrier_semaphore()
-    greeted = plane[1:] + column[1:] + [at(up, wedge), at(down, wedge)]
-    for peer in greeted:
-        pl.semaphore_signal(barrier, inc=1, device_id=peer, device_id_type=MESH)
+    signal(barrier, place, east)
+    signal(barrier, place, west)
+    pl.when(wedge < wedges // 2)(lambda: signal(barrier, place, opposite))
+    pl.when(place < last)(lambda: signal(barrier, place + 1, wedge))
+    pl.when(place > 0)(lambda: signal(barrier, place - 1, wedge))
+
+    def greet(x_start, x_stop, z_start, z_stop, semaphore):
+        def one_level(z, carry):
+            def one_group(x, inner_carry):
+                for c in range(2):
+                    signal(semaphore, x * inner + z * 2 + c, wedge)
+                return inner_carry
+
+            return lax.fori_loop(x_start, x_stop, one_group, carry)
+
+        lax.fori_loop(z_start, z_stop, one_level, 0)
+
+    greet(group + 1, groups, level, level + 1, barrier)
+    greet(0, groups, level + 1, levels, barrier)
+    greetings = (
+        2 + 2 * groups * level + 2 * group + jnp.where(wedge < wedges // 2, 0, 1)
+        + jnp.where(place > 0, 1, 0) + jnp.where(place < last, 1, 0)
+    )
 
     row = lax.broadcasted_iota(jnp.int32, (8, 128), 0)
     lane = lax.broadcasted_iota(jnp.int32, (8, 128), 1)
@@ -121,16 +166,17 @@
     tab[1] = low_face * low_face * area
     tab[2] = high_face * high_face * area
 
-    fetch_angles.wait()
-    fetch.wait()
-
+    with jax.named_scope("fetch_wait"):
+        fetch_angles.wait()
+        fetch_density.wait()
     total = u0[0, pl.ds(8, 8, stride=width), :]
     for f in range(1, width):
         total = total + u0[0, pl.ds(8 + f, 8, stride=width), :]
     shells = jnp.sum(total * ct[3:4, :], axis=1, keepdims=True) * (
         radius * radius * (radial_step * theta_step * phi_step)
     )
-    m1[0] = jnp.sum(jnp.where(lane == member * rows + row, shells, 0.0), axis=0, keepdims=True)
+    wedge_rows[0] = jnp.sum(jnp.where(lane == row, shells, 0.0), axis=0, keepdims=True)
+    fetch.wait()
 
     def pack(source, packed):
         for side, zones in enumerate(((width - 2, width - 1), (0, 1))):
@@ -139,17 +185,68 @@
                     packed[side, k, i] = source[k, pl.ds(8 + zone, 8, stride=width), :]
 
     pack(u0, pk0)
-    pl.semaphore_wait(barrier, len(greeted))
-
-    m1_copies = [
-        pltpu.make_async_remote_copy(
-            src_ref=m1.at[0], dst_ref=m1.at[j], send_sem=m1_send.at[j], recv_sem=m1_recv.at[j],
-            device_id=plane[j], device_id_type=MESH,
+    with jax.named_scope("barrier_wait"):
+        pl.semaphore_wait(barrier, greetings)
+
+    def copy_of(source, target, send, recv, radial, phi):
+        return pltpu.make_async_remote_copy(
+            src_ref=source, dst_ref=target, send_sem=send, recv_sem=recv,
+            device_id=at(radial, phi), device_id_type=MESH,
         )
-        for j in range(1, groups * wedges)
-    ]
-    for copy in m1_copies:
-        copy.start()
+
+    def mass_copy(source, x, z, c):
+        return copy_of(
+            source, shared.at[level * 2 * groups + group * 2 + core_index],
+            shared_send.at[z], shared_recv.at[level], x * inner + z * 2 + c, wedge,
+        )
+
+    def send_masses(source, x_start, z_start, z_stop):
+        def one_group(x, carry):
+            def one_level(z, inner_carry):
+                for c in range(2):
+                    mass_copy(source, x, z, c).start()
+                return inner_carry
+
+            return lax.fori_loop(z_start, z_stop, one_level, carry)
+
+        lax.fori_loop(x_start, groups, one_group, 0)
+
+    def many(count, z):
+        rows_of = shared.at[pl.ds(z * 2 * groups, count)]
+        return copy_of(rows_of, rows_of, shared_send.at[z], shared_recv.at[z], place, wedge)
+
+    def await_masses(counts, z_start, z_stop, act):
+        for x in range(groups):
+            if counts[x]:
+
+                @pl.when(group == x)
+                def _(count=counts[x]):
+                    def one_level(z, carry):
+                        act(many(count, z))
+                        return carry
+
+                    lax.fori_loop(z_start, z_stop, one_level, 0)
+
+    def wedge_copy(step):
+        return copy_of(
+            wedge_rows.at[0], wedge_rows.at[step], wedge_send, wedge_recv, place,
+            lax.rem(wedge + step, wedges),
+        )
+
+    def wedge_all():
+        others = wedge_rows.at[pl.ds(1, wedges - 1)]
+        return copy_of(others, others, wedge_send, wedge_recv, place, east)
+
+    def side_copy(side):
+        target = jnp.minimum(place + 1, last) if side == 0 else jnp.maximum(place - 1, 0)
+        return copy_of(
+            below_above.at[2], below_above.at[side], side_send.at[side], side_recv.at[side],
+            target, wedge,
+        )
+
+    for step in range(1, wedges):
+        if step != wedges // 2:
+            wedge_copy(step).start()
 
     def halo_copies(number, high_rows, low_rows, packed, radial_halo, phi_halo):
         def copy(which, source, target, peer):
@@ -159,14 +256,14 @@
             )
 
         return (
-            copy(0, high_rows, radial_halo.at[0], at(up, wedge)),
-            copy(1, low_rows, radial_halo.at[1], at(down, wedge)),
+            copy(0, high_rows, radial_halo.at[0], at(jnp.minimum(place + 1, last), wedge)),
+            copy(1, low_rows, radial_halo.at[1], at(jnp.maximum(place - 1, 0), wedge)),
             copy(2, packed.at[0], phi_halo.at[0], at(place, east)),
             copy(3, packed.at[1], phi_halo.at[1], at(place, west)),
         )
 
     def start_halos(copies, radial_halo, low_row, high_row):
-        pl.when(place < slabs - 1)(lambda: copies[0].start())
+        pl.when(place < last)(lambda: copies[0].start())
         pl.when(place > 0)(lambda: copies[1].start())
         copies[2].start()
         copies[3].start()
@@ -177,7 +274,7 @@
                 for i in range(2):
                     radial_halo[0, k, pl.ds(width * i, width), :] = low_row(k)
 
-        @pl.when(place == slabs - 1)
+        @pl.when(place == last)
         def _():
             for k in range(NV):
                 for i in range(2):
@@ -185,10 +282,10 @@
 
     def wait_radial(copies):
         pl.when(place > 0)(lambda: copies[0].wait_recv())
-        pl.when(place < slabs - 1)(lambda: copies[1].wait_recv())
+        pl.when(place < last)(lambda: copies[1].wait_recv())
 
     def wait_sent(copies):
-        pl.when(place < slabs - 1)(lambda: copies[0].wait_send())
+        pl.when(place < last)(lambda: copies[0].wait_send())
         pl.when(place > 0)(lambda: copies[1].wait_send())
         copies[2].wait_send()
         copies[3].wait_send()
@@ -203,44 +300,47 @@
         lambda k: u0[k, pl.ds(8 + (rows - 1) * width, width), :],
     )
 
+    greet(0, group, level, level + 1, from_higher)
+    greet(0, groups, 0, level, from_higher)
+    pl.when(wedge >= wedges // 2)(lambda: signal(from_opposite, place, opposite))
+
     wide_lane = lax.broadcasted_iota(jnp.int32, (width, 128), 1)
 
     def polar_and_azimuth(u):
-        def one_row(r, carry):
-            base = pl.multiple_of(8 + r * width, 8)
-            here = pl.ds(base, width)
-            cells = [u[k, here, :] for k in range(NV)]
+        def one_step(i, carry):
+            sine, inverse_sine, cotangent, mask = ct[0:1, :], ct[1:2, :], ct[2:3, :], ct[4:5, :]
+            r = jnp.maximum(i - 2, 0)
+            store = pl.ds(pl.multiple_of(r * width, 8), width)
             scale = tab[0, pl.ds(r, 1), :]
-            density = jnp.maximum(cells[0], MINIMUM_DENSITY)
-            inverse = 1.0 / density
-            speed = [None] + [cells[m] * inverse for m in (1, 2, 3)]
-            squares = cells[1] * speed[1] + cells[2] * speed[2] + cells[3] * speed[3]
-            pressure = jnp.maximum(
-                (ADIABATIC - 1.0) * (cells[4] - 0.5 * squares), PRESSURE_FLOOR * density
-            )
-            cotangent = ct[2:3, :]
-            spin = cells[3] * speed[3]
-            source = [None] * NV
-            source[1] = 2.0 * pressure + (cells[2] * speed[2] + spin)
-            source[2] = (pressure + spin) * cotangent - cells[1] * speed[2]
-            source[3] = -speed[3] * (cells[1] + cells[2] * cotangent)
-            mask = ct[4:5, :]
-            left, right = [], []
-            for k in range(NV):
-                high = (pltpu.roll(cells[k], 127, 1) - cells[k]) * mask
-                slope = half_slope(pltpu.roll(high, 1, 1), high)
-                left.append(cells[k] + slope)
-                right.append(
-                    jnp.where(wide_lane == 127, cells[k], pltpu.roll(cells[k] - slope, 127, 1))
-                )
-            flux = twice_flux(left, right, 2)
-            sine, inverse_sine = ct[0:1, :], ct[1:2, :]
-            for k in range(NV):
-                through = flux[k] * sine
+            cells = [u[k, pl.ds(pl.multiple_of(8 + r * width, 8), width), :] for k in range(NV)]
+            source = sources(cells, cotangent)
+            for k in range(NV):
+                through = th[k, store, :]
                 change = (pltpu.roll(through, 1, 1) - through) * inverse_sine
                 if source[k] is not None:
                     change = change + source[k]
-                acc[k, pl.ds(pl.multiple_of(r * width, 8), width), :] = cells[k] + scale * change
+                acc[k, store, :] = cells[k] + scale * change
+            r = jnp.clip(i - 1, 0, rows - 1)
+            store = pl.ds(pl.multiple_of(r * width, 8), width)
+            left = [lt[k, store, :] for k in range(NV)]
+            right = []
+            for k in range(NV):
+                value = rt[k, store, :]
+                cell = u[k, pl.ds(pl.multiple_of(8 + r * width, 8), width), :]
+                right.append(jnp.where(wide_lane == 127, cell, pltpu.roll(value, 127, 1)))
+            flux = twice_flux(left, right, 2)
+            for k in range(NV):
+                th[k, store, :] = flux[k] * sine
+            r = jnp.minimum(i, rows - 1)
+            base = pl.multiple_of(8 + r * width, 8)
+            store = pl.ds(pl.multiple_of(r * width, 8), width)
+            cells = [u[k, pl.ds(base, width), :] for k in range(NV)]
+            for k in range(NV):
+                high = (pltpu.roll(cells[k], 127, 1) - cells[k]) * mask
+                low = (cells[k] - pltpu.roll(cells[k], 1, 1)) * ct[5:6, :]
+                slope = half_slope(low, high)
+                lt[k, store, :] = cells[k] + slope
+                rt[k, store, :] = cells[k] - slope
             left, right = [], []
             for k in range(NV):
                 low = 0.5 * (cells[k] - u[k, pl.ds(base - 1, width), :])
@@ -253,7 +353,7 @@
                 fp[k, pl.ds(pl.multiple_of(r * span, 8), width), :] = flux[k]
             return carry
 
-        lax.fori_loop(0, rows, one_row, 0)
+        lax.fori_loop(0, rows + 2, one_step, 0)
 
     def inner_radial(u):
         def one_row(r, carry):
@@ -321,31 +421,32 @@
             )
         return values
 
-    polar_and_azimuth(u0)
-    inner_radial(u0)
-
-    for copy in m1_copies:
-        copy.wait_recv()
-    for i in range(groups):
-        shell = m1[i * wedges]
-        for j in range(1, wedges):
-            shell = shell + m1[i * wedges + j]
-        m2[0, i : i + 1, :] = shell
-    m2_copies = [
-        pltpu.make_async_remote_copy(
-            src_ref=m2.at[0], dst_ref=m2.at[j], send_sem=m2_send.at[j], recv_sem=m2_recv.at[j],
-            device_id=column[j], device_id_type=MESH,
-        )
-        for j in range(1, inner)
-    ]
-    for copy in m2_copies:
-        copy.start()
-
-    first_halos[2].wait_recv()
-    first_halos[3].wait_recv()
-    edge_azimuth(u0, hp0)
-    wait_radial(first_halos)
-    edge_radial(u0, hr0)
+    with jax.named_scope("pre1"):
+        polar_and_azimuth(u0)
+    pl.when(wedge < wedges // 2)(lambda: pl.semaphore_wait(from_opposite, 1))
+    wedge_copy(wedges // 2).start()
+    with jax.named_scope("rad1"):
+        inner_radial(u0)
+
+    with jax.named_scope("wedge_wait"):
+        wedge_all().wait_recv()
+    shell_row = wedge_rows[0]
+    for j in range(1, wedges):
+        shell_row = shell_row + wedge_rows[j]
+    below_above[2] = shell_row
+    pl.when(place < last)(lambda: side_copy(0).start())
+    pl.when(place > 0)(lambda: side_copy(1).start())
+    send_masses(below_above.at[2], group + 1, 0, level)
+
+    with jax.named_scope("h1_phi_wait"):
+        first_halos[2].wait_recv()
+        first_halos[3].wait_recv()
+    with jax.named_scope("edge_phi1"):
+        edge_azimuth(u0, hp0)
+    with jax.named_scope("h1_rad_wait"):
+        wait_radial(first_halos)
+    with jax.named_scope("edge_rad1"):
+        edge_radial(u0, hr0)
 
     def section_one_row(r, carry):
         values = advanced_row(r)
@@ -353,7 +454,8 @@
             u1[k, pl.ds(pl.multiple_of(8 + r * width, 8), width), :] = values[k]
         return carry
 
-    lax.fori_loop(0, rows, section_one_row, 0)
+    with jax.named_scope("final1"):
+        lax.fori_loop(0, rows, section_one_row, 0)
     pack(u1, pk1)
     for k in range(NV):
         sr[0, k] = u1[k, pl.ds(8 + (rows - 2) * width, 2 * width), :]
@@ -365,27 +467,58 @@
         lambda k: sr[0, k, pl.ds(width, width), :],
     )
 
-    for copy in m2_copies:
-        copy.wait_recv()
-    table = m2[0]
-    for j in range(1, inner):
-        table = table + m2[j]
-    last = slabs * rows - 1
-    beyond = jnp.clip(first + jnp.where(row < 2, row - 2, rows - 2 + row), 0, last)
-    enclosed = []
-    for target in (first + row, beyond):
-        inside = jnp.zeros((8, 128), jnp.float32)
-        for i in range(groups):
-            index = lax.rem(group + groups - i, groups) * (inner * rows) + lane
-            share = jnp.where(index < target, 1.0, jnp.where(index == target, 0.5, 0.0))
-            inside = inside + share * table[i : i + 1, :]
-        enclosed.append(jnp.sum(inside, axis=1, keepdims=True) + mass_smem[0])
+    with jax.named_scope("asc_wait"):
+        answers = 2 * groups * (levels - 1 - level) + 2 * (groups - 1 - group)
+        pl.when(answers > 0)(lambda: pl.semaphore_wait(from_higher, answers))
+    send_masses(below_above.at[2], group + 1, level, level + 1)
+    send_masses(below_above.at[2], group, level + 1, levels)
+
+    from_all = [2 * x for x in range(groups)]
+    from_lower = [2 * x + 2 for x in range(groups)]
+
+    def mass_between(z_start, z_stop, count):
+        def one_level(z, value):
+            part = shared[pl.ds(z * 2 * groups, 2 * groups)]
+            return value + jnp.sum(jnp.where(slot < count, part, 0.0), axis=0)
+
+        return lax.fori_loop(z_start, z_stop, one_level, jnp.zeros((1, 128), jnp.float32))
+
+    slot = lax.broadcasted_iota(jnp.int32, (2 * groups, 1, 128), 0)
+    with jax.named_scope("m1_wait"):
+        await_masses(from_all, level, levels, lambda copy: copy.wait_recv())
+        await_masses(from_lower, 0, level, lambda copy: copy.wait_recv())
+        pl.when(place > 0)(lambda: side_copy(0).wait_recv())
+        pl.when(place < last)(lambda: side_copy(1).wait_recv())
+    below, above, own = below_above[0], below_above[1], below_above[2]
+    half_of = lambda index: jnp.where(lane < index, 1.0, jnp.where(lane == index, 0.5, 0.0))
+    none = jnp.zeros((8, 128), jnp.float32)
+    lower = jnp.where(row < 2, jnp.where(place == 0, half_of(0), none), 0.0)
+    upper = jnp.where(row < 2, none, jnp.where(place == last, half_of(rows - 1), 1.0))
+    minus = jnp.where(lane >= rows, 0.0, half_of(rows - 2 + row) - 1.0)
+    minus = jnp.where(row < 2, minus, none)
+    plus = jnp.where(row < 2, none, half_of(row - 2))
+    inside = (
+        mass_between(level, levels, 2 * group)
+        + mass_between(0, level, 2 * group + 2)
+        + jnp.where(core_index == 1, below, 0.0)
+    )
+    table = (
+        inside + half_of(row) * own,
+        inside
+        + (lower + upper) * own
+        + jnp.where(place > 0, minus * below, none)
+        + jnp.where(place < last, plus * above, none),
+    )
+    beyond = jnp.clip(first + jnp.where(row < 2, row - 2, rows - 2 + row), 0, slabs * rows - 1)
+    fetch_mass.wait()
     for i, target in enumerate((first + row, beyond)):
+        enclosed = jnp.sum(table[i], axis=1, keepdims=True) + core[0]
         inverse = 1.0 / radius_of(target)
-        grav[8 * i : 8 * i + 8, :] = (timestep * strength) * enclosed[i] * inverse * inverse
-    enclosed_ref[...] = jnp.sum(
-        jnp.where(lane == row, enclosed[0], 0.0), axis=0, keepdims=True
-    )[:, :rows]
+        grav[8 * i : 8 * i + 8, :] = (timestep * strength) * enclosed * inverse * inverse
+        if i == 0:
+            enclosed_ref[...] = jnp.sum(
+                jnp.where(lane == row, enclosed, 0.0), axis=0, keepdims=True
+            )[:, :rows]
 
     def gravity_row(r, carry):
         base = pl.ds(pl.multiple_of(8 + r * width, 8), width)
@@ -394,12 +527,16 @@
         u1[4, base, :] = u1[4, base, :] - pull * u0[1, base, :]
         return carry
 
-    lax.fori_loop(0, rows, gravity_row, 0)
-
-    polar_and_azimuth(u1)
-    inner_radial(u1)
-    second_halos[2].wait_recv()
-    second_halos[3].wait_recv()
+    with jax.named_scope("grav"):
+        lax.fori_loop(0, rows, gravity_row, 0)
+
+    with jax.named_scope("pre2"):
+        polar_and_azimuth(u1)
+    with jax.named_scope("rad2"):
+        inner_radial(u1)
+    with jax.named_scope("h2_phi_wait"):
+        second_halos[2].wait_recv()
+        second_halos[3].wait_recv()
     pull = grav[0:8, :]
     for side in range(2):
         for i in range(2):
@@ -407,8 +544,10 @@
                 hp0[side, 0, i], MINIMUM_DENSITY
             )
             hp1[side, 4, i] = hp1[side, 4, i] - pull * hp0[side, 1, i]
-    edge_azimuth(u1, hp1)
-    wait_radial(second_halos)
+    with jax.named_scope("edge_phi2"):
+        edge_azimuth(u1, hp1)
+    with jax.named_scope("h2_rad_wait"):
+        wait_radial(second_halos)
     for side in range(2):
         for i in range(2):
             which = pl.ds(width * i, width)
@@ -417,7 +556,8 @@
                 hr0[side, 0, which, :], MINIMUM_DENSITY
             )
             hr1[side, 4, which, :] = hr1[side, 4, which, :] - pull * hr0[side, 1, which, :]
-    edge_radial(u1, hr1)
+    with jax.named_scope("edge_rad2"):
+        edge_radial(u1, hr1)
 
     def section_two_row(r, carry):
         values = advanced_row(r)
@@ -431,14 +571,29 @@
             )
         return carry
 
-    lax.fori_loop(0, rows, section_two_row, 0)
-    give = pltpu.make_async_copy(outv, out_hbm, out_sem.at[0])
-    give.start()
-    for copy in m1_copies + m2_copies:
-        copy.wait_send()
-    wait_sent(first_halos)
-    wait_sent(second_halos)
-    give.wait()
+    with jax.named_scope("final2"):
+        lax.fori_loop(0, rows, section_two_row, 0)
+    with jax.named_scope("drain"):
+        to_larger = [2 * (groups - 1 - x) for x in range(groups)]
+        to_same = [2 * (groups - x) for x in range(groups)]
+        await_masses(to_larger, 0, level + 1, lambda copy: copy.wait_send())
+        await_masses(to_same, level + 1, levels, lambda copy: copy.wait_send())
+        wedge_all().wait_send()
+        pl.when(place < last)(lambda: side_copy(0).wait_send())
+        pl.when(place > 0)(lambda: side_copy(1).wait_send())
+        wait_sent(first_halos)
+        wait_sent(second_halos)
+
+
+def put_out(advanced, enclosed, advanced_hbm, enclosed_hbm, sem):
+    copies = [
+        pltpu.make_async_copy(advanced, advanced_hbm, sem.at[0]),
+        pltpu.make_async_copy(enclosed, enclosed_hbm, sem.at[1]),
+    ]
+    for copy in copies:
+        copy.start()
+    for copy in copies:
+        copy.wait()
 
 
 def body(groups, conserved, core_mass):
@@ -454,11 +609,13 @@
     angles[2] = np.cos(centers) / np.sin(centers)
     angles[3] = np.sin(centers)
     angles[4] = np.where(np.arange(lanes) == lanes - 1, 0.0, 0.5)
+    angles[5] = np.where(np.arange(lanes) == 0, 0.0, 0.5)
     angles = jnp.asarray(angles.astype(np.float32))
     sizes = (rows, width, slabs, wedges, groups, radial_step, theta_step, phi_step, timestep)
     f32 = jnp.float32
     vmem = lambda *shape: pltpu.VMEM(shape, f32)
     dma = lambda count: pltpu.SemaphoreType.DMA((count,))
+    in_hbm = lambda value: pltpu.with_memory_space_constraint(value, pltpu.HBM)
     cells = rows * width
     advanced, enclosed = pl.pallas_call(
         functools.partial(kernel, sizes),
@@ -467,12 +624,12 @@
             jax.ShapeDtypeStruct((1, rows), f32),
         ),
         in_specs=[
-            pl.BlockSpec(memory_space=pl.ANY),
-            pl.BlockSpec(memory_space=pltpu.SMEM),
-            pl.BlockSpec(memory_space=pl.ANY),
+            pl.BlockSpec(memory_space=pltpu.HBM),
+            pl.BlockSpec(memory_space=pltpu.HBM),
+            pl.BlockSpec(memory_space=pltpu.HBM),
         ],
         out_specs=(
-            pl.BlockSpec(memory_space=pl.ANY),
+            pl.BlockSpec(memory_space=pltpu.VMEM),
             pl.BlockSpec(memory_space=pltpu.VMEM),
         ),
         scratch_shapes=[
@@ -485,14 +642,28 @@
             vmem(NV, rows * (width + 8), lanes),
             vmem(NV, cells + width, lanes),
             vmem(NV, cells, lanes),
-            vmem(NV, cells, lanes),
-            vmem(groups * wedges, 1, lanes), vmem(inner, groups, lanes),
-            vmem(3, 8, lanes), vmem(16, lanes), vmem(8, lanes),
-            dma(2), dma(1), dma(8), dma(8),
-            dma(groups * wedges), dma(groups * wedges), dma(inner), dma(inner),
+            vmem(NV, cells, lanes), vmem(NV, cells, lanes), vmem(NV, cells, lanes),
+            vmem(slabs, 1, lanes), vmem(3, 1, lanes), vmem(wedges, 1, lanes),
+            vmem(3, 8, lanes), vmem(16, lanes), vmem(8, lanes), pltpu.SMEM((1,), f32),
+            dma(4), dma(8), dma(8), dma(inner // 2), dma(inner // 2), dma(2), dma(2),
+            pltpu.SemaphoreType.DMA, pltpu.SemaphoreType.DMA,
+            pltpu.SemaphoreType.REGULAR, pltpu.SemaphoreType.REGULAR,
         ],
-        compiler_params=pltpu.CompilerParams(collective_id=0, has_side_effects=True),
-    )(conserved.reshape(NV, cells, lanes), core_mass, angles)
+        compiler_params=pltpu.CompilerParams(
+            collective_id=0, has_side_effects=True, vmem_limit_bytes=12 << 20
+        ),
+    )(in_hbm(conserved.reshape(NV, cells, lanes)), core_mass, in_hbm(angles))
+    advanced, enclosed = pl.pallas_call(
+        put_out,
+        out_shape=(
+            jax.ShapeDtypeStruct((NV, cells, lanes), f32),
+            jax.ShapeDtypeStruct((1, rows), f32),
+        ),
+        in_specs=[pl.BlockSpec(memory_space=pltpu.VMEM)] * 2,
+        out_specs=[pl.BlockSpec(memory_space=pltpu.HBM)] * 2,
+        scratch_shapes=[dma(2)],
+        compiler_params=pltpu.CompilerParams(vmem_limit_bytes=4 << 20),
+    )(advanced, enclosed)
     return advanced.reshape(conserved.shape), enclosed.reshape(rows)
 
 

time: 29.4 us -> 24.4 us (0.83)
  the two profiles are of different devices: /device:TPU:1 before, /device:TPU:7 now
where the time goes in v2:
time: 24.4 us; the launch traced here: 24.1 us
  Pallas kernels  22.8 us (93%)
  between operations  1.28 us (5%)
    pallas_call x1, Pallas kernels, body(): pl.pallas_call(functools.partial(kernel, sizes), out_shape=(jax.ShapeDtyp...  22 us
    pallas_call x1, Pallas kernels, body(): pl.pallas_call(put_out, out_shape=(jax.ShapeDtypeStruct((NV, cells, lanes...  0.81 us

profile of v2, /device:TPU:7, one launch (start us, length us, event | category | flops | bytes accessed | tf_op | source)
XLA Modules:
  0.0 24.1 jit_solution(10960160075115946160)
XLA Ops:
  1.3 22.0 %shard_map.50 = (f32[8,128,128]{2,1,0:T(8,128)S(1)}, f32[1,8]{1,0:T(1,128)S(1)}) custom-call(f32[8,128,128]{2,1,0:T(8,128)} %bitcast.3, f32[1]{0:T(128)S(6)} %copy.5.mass_hbm, f32[8,128]{1,0:T(8,128)} %constant.2.clone.angles_hbm), custom_call_target="tpu_custom_call" | custom-call | tf_op jit(solution)/shard_map/pallas_call | solution.py:620
  23.3 0.8 %shard_map.51 = (f32[8,128,128]{2,1,0:T(8,128)}, f32[1,8]{1,0:T(1,128)}) custom-call(f32[8,128,128]{2,1,0:T(8,128)S(1)} %get-tuple-element.6.advanced, f32[1,8]{1,0:T(1,128)S(1)} %get-tuple-element.7.enclosed), custom_call_target="tpu_custom_call" | custom-call | tf_op jit(solution)/shard_map/pallas_call | solution.py:656

commit v3 on v2

--- a/solution.py
+++ b/solution.py
@@ -92,7 +92,7 @@
     u0, u1, hr0, hr1, hp0, hp1, pk0, pk1, sr, acc, fp, fr, sl, lt, rt, th,
     shared, below_above, wedge_rows, tab, grav, ct, core,
     in_sem, halo_send, halo_recv, shared_send, shared_recv, side_send, side_recv,
-    wedge_send, wedge_recv, from_higher, from_opposite,
+    wedge_send, wedge_recv, from_later,
 ):
     rows, width, slabs, wedges, groups, radial_step, theta_step, phi_step, timestep = sizes
     strength = GRAVITY_KICK / timestep
@@ -112,7 +112,6 @@
         pl.semaphore_signal(semaphore, inc=1, device_id=at(radial, phi), device_id_type=MESH)
 
     east, west = lax.rem(wedge + 1, wedges), lax.rem(wedge + wedges - 1, wedges)
-    opposite = lax.rem(wedge + wedges // 2, wedges)
 
     fetch_mass = pltpu.make_async_copy(mass_hbm, core, in_sem.at[3])
     fetch_density = pltpu.make_async_copy(
@@ -127,9 +126,8 @@
         copy.start()
 
     barrier = pltpu.get_barrier_semaphore()
-    signal(barrier, place, east)
-    signal(barrier, place, west)
-    pl.when(wedge < wedges // 2)(lambda: signal(barrier, place, opposite))
+    for step in range(1, wedges):
+        signal(barrier, place, lax.rem(wedge + step, wedges))
     pl.when(place < last)(lambda: signal(barrier, place + 1, wedge))
     pl.when(place > 0)(lambda: signal(barrier, place - 1, wedge))
 
@@ -144,11 +142,41 @@
 
         lax.fori_loop(z_start, z_stop, one_level, 0)
 
-    greet(group + 1, groups, level, level + 1, barrier)
-    greet(0, groups, level + 1, levels, barrier)
+    middle = levels // 2
+    early = level < middle
+
+    def greet_after(semaphore):
+        @pl.when(early)
+        def _():
+            greet(group + 1, groups, level, level + 1, semaphore)
+            greet(0, groups, level + 1, levels, semaphore)
+
+        @pl.when(jnp.logical_not(early))
+        def _():
+            greet(group, group + 1, level + 1, levels, semaphore)
+            greet(group + 1, groups, middle, levels, semaphore)
+
+    def greet_before(semaphore):
+        @pl.when(early)
+        def _():
+            greet(0, group, level, level + 1, semaphore)
+            greet(0, groups, 0, level, semaphore)
+
+        @pl.when(jnp.logical_not(early))
+        def _():
+            greet(0, groups, 0, middle, semaphore)
+            greet(0, group, middle, levels, semaphore)
+            greet(group, group + 1, middle, level, semaphore)
+
+    before_me = 2 * jnp.where(
+        early,
+        groups * level + group,
+        groups * middle + group * (levels - middle) + level - middle,
+    )
+    after_me = 2 * (groups * levels - 1) - before_me
+    greet_after(barrier)
     greetings = (
-        2 + 2 * groups * level + 2 * group + jnp.where(wedge < wedges // 2, 0, 1)
-        + jnp.where(place > 0, 1, 0) + jnp.where(place < last, 1, 0)
+        wedges - 1 + before_me + jnp.where(place > 0, 1, 0) + jnp.where(place < last, 1, 0)
     )
 
     row = lax.broadcasted_iota(jnp.int32, (8, 128), 0)
@@ -245,8 +273,7 @@
         )
 
     for step in range(1, wedges):
-        if step != wedges // 2:
-            wedge_copy(step).start()
+        wedge_copy(step).start()
 
     def halo_copies(number, high_rows, low_rows, packed, radial_halo, phi_halo):
         def copy(which, source, target, peer):
@@ -300,9 +327,7 @@
         lambda k: u0[k, pl.ds(8 + (rows - 1) * width, width), :],
     )
 
-    greet(0, group, level, level + 1, from_higher)
-    greet(0, groups, 0, level, from_higher)
-    pl.when(wedge >= wedges // 2)(lambda: signal(from_opposite, place, opposite))
+    greet_before(from_later)
 
     wide_lane = lax.broadcasted_iota(jnp.int32, (width, 128), 1)
 
@@ -423,8 +448,6 @@
 
     with jax.named_scope("pre1"):
         polar_and_azimuth(u0)
-    pl.when(wedge < wedges // 2)(lambda: pl.semaphore_wait(from_opposite, 1))
-    wedge_copy(wedges // 2).start()
     with jax.named_scope("rad1"):
         inner_radial(u0)
 
@@ -436,7 +459,7 @@
     below_above[2] = shell_row
     pl.when(place < last)(lambda: side_copy(0).start())
     pl.when(place > 0)(lambda: side_copy(1).start())
-    send_masses(below_above.at[2], group + 1, 0, level)
+    send_masses(below_above.at[2], group + 1, 0, jnp.minimum(level, middle))
 
     with jax.named_scope("h1_phi_wait"):
         first_halos[2].wait_recv()
@@ -468,9 +491,8 @@
     )
 
     with jax.named_scope("asc_wait"):
-        answers = 2 * groups * (levels - 1 - level) + 2 * (groups - 1 - group)
-        pl.when(answers > 0)(lambda: pl.semaphore_wait(from_higher, answers))
-    send_masses(below_above.at[2], group + 1, level, level + 1)
+        pl.when(after_me > 0)(lambda: pl.semaphore_wait(from_later, after_me))
+    send_masses(below_above.at[2], group + 1, jnp.minimum(level, middle), level + 1)
     send_masses(below_above.at[2], group, level + 1, levels)
 
     from_all = [2 * x for x in range(groups)]
@@ -647,7 +669,7 @@
             vmem(3, 8, lanes), vmem(16, lanes), vmem(8, lanes), pltpu.SMEM((1,), f32),
             dma(4), dma(8), dma(8), dma(inner // 2), dma(inner // 2), dma(2), dma(2),
             pltpu.SemaphoreType.DMA, pltpu.SemaphoreType.DMA,
-            pltpu.SemaphoreType.REGULAR, pltpu.SemaphoreType.REGULAR,
+            pltpu.SemaphoreType.REGULAR,
         ],
         compiler_params=pltpu.CompilerParams(
             collective_id=0, has_side_effects=True, vmem_limit_bytes=12 << 20

time: 24.4 us -> 21.9 us (0.90)
  Pallas kernels: 22.8 us -> 20.4 us
    pallas_call x1, Pallas kernels: 22 us -> 19.6 us  [body(): pl.pallas_call(functools.partial(kernel, sizes), out_shape=(jax.ShapeDtyp...]
where the time goes in v3:
time: 21.9 us; the launch traced here: 21.7 us
  Pallas kernels  20.4 us (93%)
  between operations  1.28 us (6%)
    pallas_call x1, Pallas kernels, body(): pl.pallas_call(functools.partial(kernel, sizes), out_shape=(jax.ShapeDtyp...  19.6 us
    pallas_call x1, Pallas kernels, body(): pl.pallas_call(put_out, out_shape=(jax.ShapeDtypeStruct((NV, cells, lanes...  0.81 us

profile of v3, /device:TPU:7, one launch (start us, length us, event | category | flops | bytes accessed | tf_op | source)
XLA Modules:
  0.0 21.7 jit_solution(13999220282777761037)
XLA Ops:
  1.3 19.6 %shard_map.50 = (f32[8,128,128]{2,1,0:T(8,128)S(1)}, f32[1,8]{1,0:T(1,128)S(1)}) custom-call(f32[8,128,128]{2,1,0:T(8,128)} %bitcast.3, f32[1]{0:T(128)S(6)} %copy.5.mass_hbm, f32[8,128]{1,0:T(8,128)} %constant.2.clone.angles_hbm), custom_call_target="tpu_custom_call" | custom-call | tf_op jit(solution)/shard_map/pallas_call | solution.py:642
  20.9 0.8 %shard_map.51 = (f32[8,128,128]{2,1,0:T(8,128)}, f32[1,8]{1,0:T(1,128)}) custom-call(f32[8,128,128]{2,1,0:T(8,128)S(1)} %get-tuple-element.6.advanced, f32[1,8]{1,0:T(1,128)S(1)} %get-tuple-element.7.enclosed), custom_call_target="tpu_custom_call" | custom-call | tf_op jit(solution)/shard_map/pallas_call | solution.py:678

commit v4 on v3

--- a/solution.py
+++ b/solution.py
@@ -18,6 +18,8 @@
 PRESSURE_FLOOR = 0.01
 
 NV = 8
+STEADY = (0, 2, 3, 5, 6, 7)
+MOVED = (1, 4)
 MESH = pl.DeviceIdType.MESH
 
 
@@ -34,10 +36,13 @@
     return jnp.maximum(jnp.minimum(low, high), jnp.minimum(jnp.maximum(low, high), 0.0))
 
 
-def face_side(state, component):
+def face_side(state, component, ready=None):
     density = jnp.maximum(state[0], MINIMUM_DENSITY)
-    inverse = 1.0 / density
-    squares = state[1] * state[1] + state[2] * state[2] + state[3] * state[3]
+    if ready is None:
+        inverse, squares = 1.0 / density, state[2] * state[2] + state[3] * state[3]
+    else:
+        inverse, squares = ready
+    squares = state[1] * state[1] + squares
     pressure = jnp.maximum(
         (ADIABATIC - 1.0) * (state[4] - 0.5 * squares * inverse), PRESSURE_FLOOR * density
     )
@@ -47,9 +52,9 @@
     return pressure, normal, jnp.abs(normal) + sound
 
 
-def twice_flux(left, right, component):
-    left_p, left_v, left_s = face_side(left, component)
-    right_p, right_v, right_s = face_side(right, component)
+def twice_flux(left, right, component, ready=(None, None)):
+    left_p, left_v, left_s = face_side(left, component, ready[0])
+    right_p, right_v, right_s = face_side(right, component, ready[1])
     signal = jnp.maximum(left_s, right_s)
     left_w, right_w = left_v + signal, right_v - signal
     flux = [left[k] * left_w + right[k] * right_w for k in range(NV)]
@@ -89,7 +94,7 @@
 def kernel(
     sizes, state_hbm, mass_hbm, angles_hbm,
     outv, enclosed_ref,
-    u0, u1, hr0, hr1, hp0, hp1, pk0, pk1, sr, acc, fp, fr, sl, lt, rt, th,
+    u0, u1, hr0, hr1, hp0, hp1, pk0, pk1, sr, acc, fp, fr, sl, lt, rt, th, prep,
     shared, below_above, wedge_rows, tab, grav, ct, core,
     in_sem, halo_send, halo_recv, shared_send, shared_recv, side_send, side_recv,
     wedge_send, wedge_recv, from_later,
@@ -331,10 +336,75 @@
 
     wide_lane = lax.broadcasted_iota(jnp.int32, (width, 128), 1)
 
-    def polar_and_azimuth(u):
-        def one_step(i, carry):
-            sine, inverse_sine, cotangent, mask = ct[0:1, :], ct[1:2, :], ct[2:3, :], ct[4:5, :]
-            r = jnp.maximum(i - 2, 0)
+    def keep(direction, side, where, state):
+        for n, k in enumerate(STEADY):
+            prep[direction, side, n, where, :] = state[k]
+        prep[direction, side, len(STEADY), where, :] = 1.0 / jnp.maximum(
+            state[0], MINIMUM_DENSITY
+        )
+        prep[direction, side, len(STEADY) + 1, where, :] = (
+            state[2] * state[2] + state[3] * state[3]
+        )
+
+    def kept(direction, where, left, right):
+        ready = []
+        for side, state in enumerate((left, right)):
+            for n, k in enumerate(STEADY):
+                state[k] = prep[direction, side, n, where, :]
+            ready.append(tuple(prep[direction, side, len(STEADY) + n, where, :] for n in (0, 1)))
+        return ready
+
+    def prepare(u):
+        def one_row(r, carry):
+            base = pl.multiple_of(8 + r * width, 8)
+            where = pl.ds(pl.multiple_of(r * width, 8), width)
+            left, right = {}, {}
+            for k in STEADY:
+                cell = u[k, pl.ds(base, width), :]
+                high = (pltpu.roll(cell, 127, 1) - cell) * ct[4:5, :]
+                low = (cell - pltpu.roll(cell, 1, 1)) * ct[5:6, :]
+                slope = half_slope(low, high)
+                left[k] = cell + slope
+                right[k] = jnp.where(wide_lane == 127, cell, pltpu.roll(cell - slope, 127, 1))
+            keep(0, 0, where, left)
+            keep(0, 1, where, right)
+            for k in STEADY:
+                cell = u[k, pl.ds(base, width), :]
+                low = 0.5 * (cell - u[k, pl.ds(base - 1, width), :])
+                high = 0.5 * (u[k, pl.ds(base + 1, width), :] - cell)
+                slope = half_slope(low, high)
+                left[k] = pltpu.roll(cell + slope, 1, 0)
+                right[k] = cell - slope
+            keep(1, 0, where, left)
+            keep(1, 1, where, right)
+            return carry
+
+        lax.fori_loop(0, rows, one_row, 0)
+
+        def one_inner_row(r, carry):
+            base = pl.multiple_of(8 + r * width, 8)
+            where = pl.multiple_of(r * width, 8)
+            left, right = {}, {}
+            for k in STEADY:
+                cell = u[k, pl.ds(base, width), :]
+                low = 0.5 * (cell - u[k, pl.ds(base - width, width), :])
+                high = 0.5 * (u[k, pl.ds(base + width, width), :] - cell)
+                slope = half_slope(low, high)
+                left[k], right[k] = cell + slope, cell - slope
+            keep(2, 0, pl.ds(pl.multiple_of(where + width, 8), width), left)
+            keep(2, 1, pl.ds(where, width), right)
+            return carry
+
+        lax.fori_loop(1, rows - 1, one_inner_row, 0)
+
+    def polar_and_azimuth(u, prepared=False):
+        moving = MOVED if prepared else range(NV)
+
+        together = 2 if prepared else 1
+        sine, inverse_sine, cotangent, mask = ct[0:1, :], ct[1:2, :], ct[2:3, :], ct[4:5, :]
+
+        def third(i, n):
+            r = jnp.maximum((i - 2) * together, 0) + n
             store = pl.ds(pl.multiple_of(r * width, 8), width)
             scale = tab[0, pl.ds(r, 1), :]
             cells = [u[k, pl.ds(pl.multiple_of(8 + r * width, 8), width), :] for k in range(NV)]
@@ -345,56 +415,69 @@
                 if source[k] is not None:
                     change = change + source[k]
                 acc[k, store, :] = cells[k] + scale * change
-            r = jnp.clip(i - 1, 0, rows - 1)
+
+        def second(i, n):
+            r = jnp.clip((i - 1) * together, 0, rows - together) + n
             store = pl.ds(pl.multiple_of(r * width, 8), width)
-            left = [lt[k, store, :] for k in range(NV)]
-            right = []
-            for k in range(NV):
+            left = {k: lt[k, store, :] for k in moving}
+            right = {}
+            for k in moving:
                 value = rt[k, store, :]
                 cell = u[k, pl.ds(pl.multiple_of(8 + r * width, 8), width), :]
-                right.append(jnp.where(wide_lane == 127, cell, pltpu.roll(value, 127, 1)))
-            flux = twice_flux(left, right, 2)
+                right[k] = jnp.where(wide_lane == 127, cell, pltpu.roll(value, 127, 1))
+            ready = kept(0, store, left, right) if prepared else (None, None)
+            flux = twice_flux(left, right, 2, ready)
             for k in range(NV):
                 th[k, store, :] = flux[k] * sine
-            r = jnp.minimum(i, rows - 1)
+
+        def first(i, n):
+            r = jnp.minimum(i * together, rows - together) + n
             base = pl.multiple_of(8 + r * width, 8)
             store = pl.ds(pl.multiple_of(r * width, 8), width)
-            cells = [u[k, pl.ds(base, width), :] for k in range(NV)]
-            for k in range(NV):
+            cells = {k: u[k, pl.ds(base, width), :] for k in moving}
+            for k in moving:
                 high = (pltpu.roll(cells[k], 127, 1) - cells[k]) * mask
                 low = (cells[k] - pltpu.roll(cells[k], 1, 1)) * ct[5:6, :]
                 slope = half_slope(low, high)
                 lt[k, store, :] = cells[k] + slope
                 rt[k, store, :] = cells[k] - slope
-            left, right = [], []
-            for k in range(NV):
+            left, right = {}, {}
+            for k in moving:
                 low = 0.5 * (cells[k] - u[k, pl.ds(base - 1, width), :])
                 high = 0.5 * (u[k, pl.ds(base + 1, width), :] - cells[k])
                 slope = half_slope(low, high)
-                left.append(pltpu.roll(cells[k] + slope, 1, 0))
-                right.append(cells[k] - slope)
-            flux = twice_flux(left, right, 3)
+                left[k] = pltpu.roll(cells[k] + slope, 1, 0)
+                right[k] = cells[k] - slope
+            ready = kept(1, store, left, right) if prepared else (None, None)
+            flux = twice_flux(left, right, 3, ready)
             for k in range(NV):
                 fp[k, pl.ds(pl.multiple_of(r * span, 8), width), :] = flux[k]
+
+        def one_step(i, carry):
+            for stage in (third, second, first):
+                for n in range(together):
+                    stage(i, n)
             return carry
 
-        lax.fori_loop(0, rows + 2, one_step, 0)
-
-    def inner_radial(u):
+        lax.fori_loop(0, rows // together + 2, one_step, 0)
+
+    def inner_radial(u, prepared=False):
+        moving = MOVED if prepared else range(NV)
+
         def one_row(r, carry):
             base = pl.multiple_of(8 + r * width, 8)
             store = pl.multiple_of(r * width, 8)
-            right = []
-            left = []
-            for k in range(NV):
+            left, right = {}, {}
+            for k in moving:
                 cell = u[k, pl.ds(base, width), :]
                 low = 0.5 * (cell - u[k, pl.ds(base - width, width), :])
                 high = 0.5 * (u[k, pl.ds(base + width, width), :] - cell)
                 slope = half_slope(low, high)
-                right.append(cell - slope)
-                left.append(sl[k, pl.ds(store - width, width), :])
+                right[k] = cell - slope
+                left[k] = sl[k, pl.ds(store - width, width), :]
                 sl[k, pl.ds(store, width), :] = cell + slope
-            flux = twice_flux(left, right, 1)
+            ready = kept(2, pl.ds(store, width), left, right) if prepared else (None, None)
+            flux = twice_flux(left, right, 1, ready)
             for k in range(NV):
                 fr[k, pl.ds(store, width), :] = flux[k]
             return carry
@@ -506,6 +589,8 @@
         return lax.fori_loop(z_start, z_stop, one_level, jnp.zeros((1, 128), jnp.float32))
 
     slot = lax.broadcasted_iota(jnp.int32, (2 * groups, 1, 128), 0)
+    with jax.named_scope("prepare"):
+        prepare(u1)
     with jax.named_scope("m1_wait"):
         await_masses(from_all, level, levels, lambda copy: copy.wait_recv())
         await_masses(from_lower, 0, level, lambda copy: copy.wait_recv())
@@ -553,9 +638,9 @@
         lax.fori_loop(0, rows, gravity_row, 0)
 
     with jax.named_scope("pre2"):
-        polar_and_azimuth(u1)
+        polar_and_azimuth(u1, prepared=True)
     with jax.named_scope("rad2"):
-        inner_radial(u1)
+        inner_radial(u1, prepared=True)
     with jax.named_scope("h2_phi_wait"):
         second_halos[2].wait_recv()
         second_halos[3].wait_recv()
@@ -665,6 +750,7 @@
             vmem(NV, cells + width, lanes),
             vmem(NV, cells, lanes),
             vmem(NV, cells, lanes), vmem(NV, cells, lanes), vmem(NV, cells, lanes),
+            vmem(3, 2, len(STEADY) + 2, cells, lanes),
             vmem(slabs, 1, lanes), vmem(3, 1, lanes), vmem(wedges, 1, lanes),
             vmem(3, 8, lanes), vmem(16, lanes), vmem(8, lanes), pltpu.SMEM((1,), f32),
             dma(4), dma(8), dma(8), dma(inner // 2), dma(inner // 2), dma(2), dma(2),

time: 21.9 us -> 21.7 us (level)
  the two profiles are of different devices: /device:TPU:7 before, /device:TPU:2 now
where the time goes in v4:
time: 21.7 us; the launch traced here: 21.6 us
  Pallas kernels  20.3 us (94%)
  between operations  1.28 us (6%)
    pallas_call x1, Pallas kernels, body(): pl.pallas_call(functools.partial(kernel, sizes), out_shape=(jax.ShapeDtyp...  19.5 us
    pallas_call x1, Pallas kernels, body(): pl.pallas_call(put_out, out_shape=(jax.ShapeDtypeStruct((NV, cells, lanes...  0.81 us

profile of v4, /device:TPU:2, one launch (start us, length us, event | category | flops | bytes accessed | tf_op | source)
XLA Modules:
  0.0 21.6 jit_solution(18261850554616845448)
XLA Ops:
  1.3 19.5 %shard_map.50 = (f32[8,128,128]{2,1,0:T(8,128)S(1)}, f32[1,8]{1,0:T(1,128)S(1)}) custom-call(f32[8,128,128]{2,1,0:T(8,128)} %bitcast.3, f32[1]{0:T(128)S(6)} %copy.5.mass_hbm, f32[8,128]{1,0:T(8,128)} %constant.2.clone.angles_hbm), custom_call_target="tpu_custom_call" | custom-call | tf_op jit(solution)/shard_map/pallas_call | solution.py:727
  20.8 0.8 %shard_map.51 = (f32[8,128,128]{2,1,0:T(8,128)}, f32[1,8]{1,0:T(1,128)}) custom-call(f32[8,128,128]{2,1,0:T(8,128)S(1)} %get-tuple-element.6.advanced, f32[1,8]{1,0:T(1,128)S(1)} %get-tuple-element.7.enclosed), custom_call_target="tpu_custom_call" | custom-call | tf_op jit(solution)/shard_map/pallas_call | solution.py:764

commit v5 on v4

--- a/solution.py
+++ b/solution.py
@@ -95,9 +95,10 @@
     sizes, state_hbm, mass_hbm, angles_hbm,
     outv, enclosed_ref,
     u0, u1, hr0, hr1, hp0, hp1, pk0, pk1, sr, acc, fp, fr, sl, lt, rt, th, prep,
-    shared, below_above, wedge_rows, tab, grav, ct, core,
-    in_sem, halo_send, halo_recv, shared_send, shared_recv, side_send, side_recv,
-    wedge_send, wedge_recv, from_later,
+    shared, along, below_above, wedge_rows, chip_rows, inside_rows, weights, tab, grav, ct, core,
+    in_sem, halo_send, halo_recv, shared_send, shared_recv, along_send, along_recv,
+    side_send, side_recv, pass_send, pass_recv, wedge_send, wedge_recv, chip_send, chip_recv,
+    from_near, from_far,
 ):
     rows, width, slabs, wedges, groups, radial_step, theta_step, phi_step, timestep = sizes
     strength = GRAVITY_KICK / timestep
@@ -130,16 +131,21 @@
     for copy in (fetch_density, fetch_angles, fetch, fetch_mass):
         copy.start()
 
+    for side in range(2):
+        below_above[side] = jnp.zeros((1, 128), jnp.float32)
+
     barrier = pltpu.get_barrier_semaphore()
     for step in range(1, wedges):
         signal(barrier, place, lax.rem(wedge + step, wedges))
     pl.when(place < last)(lambda: signal(barrier, place + 1, wedge))
     pl.when(place > 0)(lambda: signal(barrier, place - 1, wedge))
 
-    def greet(x_start, x_stop, z_start, z_stop, semaphore):
-        def one_level(z, carry):
+    def greet(x_start, x_stop, z_start, z_stop, cores, semaphore):
+        def one_level(back, carry):
+            z = z_start + z_stop - 1 - back
+
             def one_group(x, inner_carry):
-                for c in range(2):
+                for c in cores:
                     signal(semaphore, x * inner + z * 2 + c, wedge)
                 return inner_carry
 
@@ -147,41 +153,32 @@
 
         lax.fori_loop(z_start, z_stop, one_level, 0)
 
-    middle = levels // 2
-    early = level < middle
-
-    def greet_after(semaphore):
-        @pl.when(early)
-        def _():
-            greet(group + 1, groups, level, level + 1, semaphore)
-            greet(0, groups, level + 1, levels, semaphore)
-
-        @pl.when(jnp.logical_not(early))
-        def _():
-            greet(group, group + 1, level + 1, levels, semaphore)
-            greet(group + 1, groups, middle, levels, semaphore)
-
-    def greet_before(semaphore):
-        @pl.when(early)
-        def _():
-            greet(0, group, level, level + 1, semaphore)
-            greet(0, groups, 0, level, semaphore)
-
-        @pl.when(jnp.logical_not(early))
-        def _():
-            greet(0, groups, 0, middle, semaphore)
-            greet(0, group, middle, levels, semaphore)
-            greet(group, group + 1, middle, level, semaphore)
-
-    before_me = 2 * jnp.where(
-        early,
-        groups * level + group,
-        groups * middle + group * (levels - middle) + level - middle,
-    )
-    after_me = 2 * (groups * levels - 1) - before_me
-    greet_after(barrier)
+    near = levels // 4
+    is_near = level < near
+    sender = core_index == 1
+    both = (0, 1)
+
+    pl.when(is_near)(lambda: greet(0, group, level + 1, levels, (1,), barrier))
+
+    @pl.when(sender)
+    def _():
+        for step in range(1, wedges):
+            signal(barrier, place - 1, lax.rem(wedge + step, wedges))
+        greet(group, group + 1, level + 1, levels, both, barrier)
+        pl.when(is_near)(lambda: greet(group + 1, groups, level, near, both, barrier))
+
+    def answer():
+        greet(group, group + 1, 0, level, (1,), from_far)
+        pl.when(is_near)(lambda: greet(0, group, 0, level + 1, (1,), from_near))
+
+    near_answers = jnp.where(
+        jnp.logical_and(sender, is_near), 2 * (groups - 1 - group) * (near - level), 0
+    )
+    far_answers = jnp.where(sender, 2 * (levels - 1 - level), 0)
     greetings = (
-        wedges - 1 + before_me + jnp.where(place > 0, 1, 0) + jnp.where(place < last, 1, 0)
+        wedges - 1 + jnp.where(place > 0, 1, 0) + jnp.where(place < last, 1, 0) + level
+        + jnp.where(is_near, group * (level + 1), 0)
+        + jnp.where(sender, 2 * (groups - 1 - group) * jnp.minimum(level, near), wedges - 1)
     )
 
     row = lax.broadcasted_iota(jnp.int32, (8, 128), 0)
@@ -227,38 +224,51 @@
             device_id=at(radial, phi), device_id_type=MESH,
         )
 
-    def mass_copy(source, x, z, c):
-        return copy_of(
-            source, shared.at[level * 2 * groups + group * 2 + core_index],
-            shared_send.at[z], shared_recv.at[level], x * inner + z * 2 + c, wedge,
-        )
-
-    def send_masses(source, x_start, z_start, z_stop):
+    def send_across(z_start, z_stop):
         def one_group(x, carry):
             def one_level(z, inner_carry):
-                for c in range(2):
-                    mass_copy(source, x, z, c).start()
+                for c in both:
+                    copy_of(
+                        below_above.at[3], shared.at[level * groups + group], shared_send.at[z],
+                        shared_recv.at[level], x * inner + z * 2 + c, wedge,
+                    ).start()
                 return inner_carry
 
             return lax.fori_loop(z_start, z_stop, one_level, carry)
 
-        lax.fori_loop(x_start, groups, one_group, 0)
-
-    def many(count, z):
-        rows_of = shared.at[pl.ds(z * 2 * groups, count)]
-        return copy_of(rows_of, rows_of, shared_send.at[z], shared_recv.at[z], place, wedge)
-
-    def await_masses(counts, z_start, z_stop, act):
-        for x in range(groups):
-            if counts[x]:
-
-                @pl.when(group == x)
-                def _(count=counts[x]):
-                    def one_level(z, carry):
-                        act(many(count, z))
-                        return carry
-
-                    lax.fori_loop(z_start, z_stop, one_level, 0)
+        lax.fori_loop(group + 1, groups, one_group, 0)
+
+    def send_along():
+        def one_level(z, carry):
+            for c in both:
+                copy_of(
+                    below_above.at[3], along.at[level], along_send.at[z], along_recv.at[level],
+                    group * inner + z * 2 + c, wedge,
+                ).start()
+            return carry
+
+        lax.fori_loop(level + 1, levels, one_level, 0)
+
+    def many(count, send, recv):
+        rows_of = shared.at[pl.ds(0, count)]
+        return copy_of(rows_of, rows_of, send, recv, place, wedge)
+
+    passers = (
+        (near - 1, near, near + (levels - near + 1) // 2),
+        (0, near + (levels - near + 1) // 2, levels),
+    )
+
+    def pass_copy(z, c):
+        return copy_of(
+            inside_rows.at[0], inside_rows.at[1], pass_send, pass_recv,
+            group * inner + z * 2 + c, wedge,
+        )
+
+    def chip_copy(step):
+        return copy_of(
+            wedge_rows.at[0], chip_rows.at[step], chip_send, chip_recv,
+            jnp.minimum(place + 1, last), lax.rem(wedge + step, wedges),
+        )
 
     def wedge_copy(step):
         return copy_of(
@@ -277,6 +287,11 @@
             target, wedge,
         )
 
+    @pl.when(jnp.logical_not(sender))
+    def _():
+        for step in range(wedges):
+            chip_copy(step).start()
+
     for step in range(1, wedges):
         wedge_copy(step).start()
 
@@ -332,7 +347,7 @@
         lambda k: u0[k, pl.ds(8 + (rows - 1) * width, width), :],
     )
 
-    greet_before(from_later)
+    answer()
 
     wide_lane = lax.broadcasted_iota(jnp.int32, (width, 128), 1)
 
@@ -453,13 +468,24 @@
             for k in range(NV):
                 fp[k, pl.ds(pl.multiple_of(r * span, 8), width), :] = flux[k]
 
-        def one_step(i, carry):
-            for stage in (third, second, first):
+        def run(i, stages):
+            for stage in stages:
                 for n in range(together):
                     stage(i, n)
+
+        def one_step(i, carry):
+            run(i, (third, second, first))
             return carry
 
-        lax.fori_loop(0, rows // together + 2, one_step, 0)
+        steps = rows // together
+        if prepared:
+            run(0, (first,))
+            run(1, (second, first))
+            lax.fori_loop(2, steps, one_step, 0)
+            run(steps, (third, second))
+            run(steps + 1, (third,))
+        else:
+            lax.fori_loop(0, steps + 2, one_step, 0)
 
     def inner_radial(u, prepared=False):
         moving = MOVED if prepared else range(NV)
@@ -542,7 +568,17 @@
     below_above[2] = shell_row
     pl.when(place < last)(lambda: side_copy(0).start())
     pl.when(place > 0)(lambda: side_copy(1).start())
-    send_masses(below_above.at[2], group + 1, 0, jnp.minimum(level, middle))
+
+    @pl.when(sender)
+    def _():
+        many(wedges, chip_send, chip_recv).wait_recv()
+        chip_row = shell_row
+        for j in range(wedges):
+            chip_row = chip_row + chip_rows[j]
+        below_above[3] = chip_row
+        send_across(0, jnp.minimum(level, near))
+        pl.when(near_answers > 0)(lambda: pl.semaphore_wait(from_near, near_answers))
+        send_across(jnp.minimum(level, near), near)
 
     with jax.named_scope("h1_phi_wait"):
         first_halos[2].wait_recv()
@@ -574,54 +610,75 @@
     )
 
     with jax.named_scope("asc_wait"):
-        pl.when(after_me > 0)(lambda: pl.semaphore_wait(from_later, after_me))
-    send_masses(below_above.at[2], group + 1, jnp.minimum(level, middle), level + 1)
-    send_masses(below_above.at[2], group, level + 1, levels)
-
-    from_all = [2 * x for x in range(groups)]
-    from_lower = [2 * x + 2 for x in range(groups)]
-
-    def mass_between(z_start, z_stop, count):
+        pl.when(far_answers > 0)(lambda: pl.semaphore_wait(from_far, far_answers))
+    pl.when(sender)(send_along)
+
+    def gather_across():
+        for x in range(1, groups):
+
+            @pl.when(group == x)
+            def _(count=x):
+                def one_level(z, value):
+                    many(count, shared_send.at[0], shared_recv.at[z]).wait_recv()
+                    for n in range(count):
+                        value = value + shared[z * groups + n]
+                    return value
+
+                inside_rows[0] = lax.fori_loop(
+                    0, levels, one_level, jnp.zeros((1, 128), jnp.float32)
+                )
+                for passer, z_start, z_stop in passers:
+
+                    @pl.when(jnp.logical_and(sender, level == passer))
+                    def _(z_start=z_start, z_stop=z_stop):
+                        for z in range(z_start, z_stop):
+                            for c in both:
+                                pass_copy(z, c).start()
+
+    def gather_along():
         def one_level(z, value):
-            part = shared[pl.ds(z * 2 * groups, 2 * groups)]
-            return value + jnp.sum(jnp.where(slot < count, part, 0.0), axis=0)
-
-        return lax.fori_loop(z_start, z_stop, one_level, jnp.zeros((1, 128), jnp.float32))
-
-    slot = lax.broadcasted_iota(jnp.int32, (2 * groups, 1, 128), 0)
-    with jax.named_scope("prepare"):
-        prepare(u1)
-    with jax.named_scope("m1_wait"):
-        await_masses(from_all, level, levels, lambda copy: copy.wait_recv())
-        await_masses(from_lower, 0, level, lambda copy: copy.wait_recv())
-        pl.when(place > 0)(lambda: side_copy(0).wait_recv())
-        pl.when(place < last)(lambda: side_copy(1).wait_recv())
-    below, above, own = below_above[0], below_above[1], below_above[2]
+            many(1, along_send.at[0], along_recv.at[z]).wait_recv()
+            return value + along[z]
+
+        return lax.fori_loop(0, level, one_level, jnp.zeros((1, 128), jnp.float32))
+
     half_of = lambda index: jnp.where(lane < index, 1.0, jnp.where(lane == index, 0.5, 0.0))
     none = jnp.zeros((8, 128), jnp.float32)
     lower = jnp.where(row < 2, jnp.where(place == 0, half_of(0), none), 0.0)
     upper = jnp.where(row < 2, none, jnp.where(place == last, half_of(rows - 1), 1.0))
     minus = jnp.where(lane >= rows, 0.0, half_of(rows - 2 + row) - 1.0)
-    minus = jnp.where(row < 2, minus, none)
-    plus = jnp.where(row < 2, none, half_of(row - 2))
-    inside = (
-        mass_between(level, levels, 2 * group)
-        + mass_between(0, level, 2 * group + 2)
-        + jnp.where(core_index == 1, below, 0.0)
-    )
+    minus = jnp.where(jnp.logical_and(row < 2, place > 0), minus, none)
+    plus = jnp.where(jnp.logical_or(row < 2, place == last), none, half_of(row - 2))
+    beyond = jnp.clip(first + jnp.where(row < 2, row - 2, rows - 2 + row), 0, slabs * rows - 1)
+    weights[0] = half_of(row)
+    weights[1] = lower + upper
+    weights[2] = minus
+    weights[3] = plus
+    for i, target in enumerate((first + row, beyond)):
+        inverse = 1.0 / radius_of(target)
+        weights[4 + i] = (timestep * strength) * inverse * inverse
+    fetch_mass.wait()
+
+    with jax.named_scope("prepare"):
+        prepare(u1)
+    with jax.named_scope("m1_wait"):
+        pl.when(is_near)(gather_across)
+        inside = gather_along()
+        pl.when(jnp.logical_and(group > 0, jnp.logical_not(is_near)))(
+            lambda: pass_copy(levels - 1, 1).wait_recv()
+        )
+        pl.when(place > 0)(lambda: side_copy(0).wait_recv())
+        pl.when(place < last)(lambda: side_copy(1).wait_recv())
+    below, above, own = below_above[0], below_above[1], below_above[2]
+    smaller_x = jnp.where(is_near, inside_rows[0], inside_rows[1])
+    inside = inside + jnp.where(group > 0, smaller_x, 0.0) + jnp.where(core_index == 1, below, 0.0)
     table = (
-        inside + half_of(row) * own,
-        inside
-        + (lower + upper) * own
-        + jnp.where(place > 0, minus * below, none)
-        + jnp.where(place < last, plus * above, none),
-    )
-    beyond = jnp.clip(first + jnp.where(row < 2, row - 2, rows - 2 + row), 0, slabs * rows - 1)
-    fetch_mass.wait()
-    for i, target in enumerate((first + row, beyond)):
+        inside + weights[0] * own,
+        inside + weights[1] * own + weights[2] * below + weights[3] * above,
+    )
+    for i in range(2):
         enclosed = jnp.sum(table[i], axis=1, keepdims=True) + core[0]
-        inverse = 1.0 / radius_of(target)
-        grav[8 * i : 8 * i + 8, :] = (timestep * strength) * enclosed * inverse * inverse
+        grav[8 * i : 8 * i + 8, :] = weights[4 + i] * enclosed
         if i == 0:
             enclosed_ref[...] = jnp.sum(
                 jnp.where(lane == row, enclosed, 0.0), axis=0, keepdims=True
@@ -681,10 +738,28 @@
     with jax.named_scope("final2"):
         lax.fori_loop(0, rows, section_two_row, 0)
     with jax.named_scope("drain"):
-        to_larger = [2 * (groups - 1 - x) for x in range(groups)]
-        to_same = [2 * (groups - x) for x in range(groups)]
-        await_masses(to_larger, 0, level + 1, lambda copy: copy.wait_send())
-        await_masses(to_same, level + 1, levels, lambda copy: copy.wait_send())
+        @pl.when(sender)
+        def _():
+            for x in range(groups - 1):
+
+                @pl.when(group == x)
+                def _(count=2 * (groups - 1 - x)):
+                    for z in range(near):
+                        many(count, shared_send.at[z], shared_recv.at[0]).wait_send()
+
+            def sent_along(z, carry):
+                many(2, along_send.at[z], along_recv.at[0]).wait_send()
+                return carry
+
+            lax.fori_loop(level + 1, levels, sent_along, 0)
+            for passer, z_start, z_stop in passers:
+                pl.when(jnp.logical_and(group > 0, level == passer))(
+                    lambda count=2 * (z_stop - z_start): many(
+                        count, pass_send, pass_recv
+                    ).wait_send()
+                )
+
+        pl.when(jnp.logical_not(sender))(lambda: many(wedges, chip_send, chip_recv).wait_send())
         wedge_all().wait_send()
         pl.when(place < last)(lambda: side_copy(0).wait_send())
         pl.when(place > 0)(lambda: side_copy(1).wait_send())
@@ -694,9 +769,8 @@
 
 def put_out(advanced, enclosed, advanced_hbm, enclosed_hbm, sem):
     copies = [
-        pltpu.make_async_copy(advanced, advanced_hbm, sem.at[0]),
-        pltpu.make_async_copy(enclosed, enclosed_hbm, sem.at[1]),
-    ]
+        pltpu.make_async_copy(advanced.at[k], advanced_hbm.at[k], sem.at[k]) for k in range(NV)
+    ] + [pltpu.make_async_copy(enclosed, enclosed_hbm, sem.at[NV])]
     for copy in copies:
         copy.start()
     for copy in copies:
@@ -751,11 +825,15 @@
             vmem(NV, cells, lanes),
             vmem(NV, cells, lanes), vmem(NV, cells, lanes), vmem(NV, cells, lanes),
             vmem(3, 2, len(STEADY) + 2, cells, lanes),
-            vmem(slabs, 1, lanes), vmem(3, 1, lanes), vmem(wedges, 1, lanes),
+            vmem(slabs // 2, 1, lanes), vmem(inner // 2, 1, lanes), vmem(4, 1, lanes), vmem(wedges, 1, lanes),
+            vmem(wedges, 1, lanes), vmem(2, 1, lanes), vmem(6, 8, lanes),
             vmem(3, 8, lanes), vmem(16, lanes), vmem(8, lanes), pltpu.SMEM((1,), f32),
-            dma(4), dma(8), dma(8), dma(inner // 2), dma(inner // 2), dma(2), dma(2),
+            dma(4), dma(8), dma(8), dma(inner // 8), dma(inner // 2),
+            dma(inner // 2), dma(inner // 2), dma(2), dma(2),
             pltpu.SemaphoreType.DMA, pltpu.SemaphoreType.DMA,
-            pltpu.SemaphoreType.REGULAR,
+            pltpu.SemaphoreType.DMA, pltpu.SemaphoreType.DMA,
+            pltpu.SemaphoreType.DMA, pltpu.SemaphoreType.DMA,
+            pltpu.SemaphoreType.REGULAR, pltpu.SemaphoreType.REGULAR,
         ],
         compiler_params=pltpu.CompilerParams(
             collective_id=0, has_side_effects=True, vmem_limit_bytes=12 << 20
@@ -769,7 +847,7 @@
         ),
         in_specs=[pl.BlockSpec(memory_space=pltpu.VMEM)] * 2,
         out_specs=[pl.BlockSpec(memory_space=pltpu.HBM)] * 2,
-        scratch_shapes=[dma(2)],
+        scratch_shapes=[dma(NV + 1)],
         compiler_params=pltpu.CompilerParams(vmem_limit_bytes=4 << 20),
     )(advanced, enclosed)
     return advanced.reshape(conserved.shape), enclosed.reshape(rows)

time: 21.7 us -> 19.7 us (0.908)
  the two profiles are of different devices: /device:TPU:2 before, /device:TPU:7 now
where the time goes in v5:
time: 19.7 us; the launch traced here: 19.6 us
  Pallas kernels  18.3 us (93%)
  between operations  1.28 us (6%)
    pallas_call x1, Pallas kernels, body(): pl.pallas_call(functools.partial(kernel, sizes), out_shape=(jax.ShapeDtyp...  17.4 us
    pallas_call x1, Pallas kernels, body(): pl.pallas_call(put_out, out_shape=(jax.ShapeDtypeStruct((NV, cells, lanes...  0.86 us

profile of v5, /device:TPU:7, one launch (start us, length us, event | category | flops | bytes accessed | tf_op | source)
XLA Modules:
  0.0 19.6 jit_solution(13742642766638077026)
XLA Ops:
  1.3 17.4 %shard_map.50 = (f32[8,128,128]{2,1,0:T(8,128)S(1)}, f32[1,8]{1,0:T(1,128)S(1)}) custom-call(f32[8,128,128]{2,1,0:T(8,128)} %bitcast.3, f32[1]{0:T(128)S(6)} %copy.5.mass_hbm, f32[8,128]{1,0:T(8,128)} %constant.2.clone.angles_hbm), custom_call_target="tpu_custom_call" | custom-call | tf_op jit(solution)/shard_map/pallas_call | solution.py:801
  18.7 0.9 %shard_map.51 = (f32[8,128,128]{2,1,0:T(8,128)}, f32[1,8]{1,0:T(1,128)}) custom-call(f32[8,128,128]{2,1,0:T(8,128)S(1)} %get-tuple-element.6.advanced, f32[1,8]{1,0:T(1,128)S(1)} %get-tuple-element.7.enclosed), custom_call_target="tpu_custom_call" | custom-call | tf_op jit(solution)/shard_map/pallas_call | solution.py:842

commit v6 on v5

--- a/solution.py
+++ b/solution.py
@@ -36,27 +36,32 @@
     return jnp.maximum(jnp.minimum(low, high), jnp.minimum(jnp.maximum(low, high), 0.0))
 
 
+def side_ready(state):
+    density = jnp.maximum(state[0], MINIMUM_DENSITY)
+    squares = state[2] * state[2] + state[3] * state[3]
+    return 1.0 / density, squares, PRESSURE_FLOOR * density
+
+
 def face_side(state, component, ready=None):
-    density = jnp.maximum(state[0], MINIMUM_DENSITY)
     if ready is None:
-        inverse, squares = 1.0 / density, state[2] * state[2] + state[3] * state[3]
-    else:
-        inverse, squares = ready
+        ready = side_ready(state)
+    inverse, squares, floor = ready
     squares = state[1] * state[1] + squares
-    pressure = jnp.maximum(
-        (ADIABATIC - 1.0) * (state[4] - 0.5 * squares * inverse), PRESSURE_FLOOR * density
-    )
+    pressure = jnp.maximum((ADIABATIC - 1.0) * (state[4] - 0.5 * squares * inverse), floor)
     normal = state[component] * inverse
     square = ADIABATIC * pressure * inverse
     sound = square * lax.rsqrt(square)
     return pressure, normal, jnp.abs(normal) + sound
 
 
-def twice_flux(left, right, component, ready=(None, None)):
+def twice_flux(left, right, component, ready=(None, None), factor=None):
     left_p, left_v, left_s = face_side(left, component, ready[0])
     right_p, right_v, right_s = face_side(right, component, ready[1])
     signal = jnp.maximum(left_s, right_s)
     left_w, right_w = left_v + signal, right_v - signal
+    if factor is not None:
+        left_w, right_w = left_w * factor, right_w * factor
+        left_p, right_p = left_p * factor, right_p * factor
     flux = [left[k] * left_w + right[k] * right_w for k in range(NV)]
     flux[component] = flux[component] + (left_p + right_p)
     flux[4] = flux[4] + (left_p * left_v + right_p * right_v)
@@ -73,6 +78,15 @@
     return [
         twice_flux([a[i] for a in lefts], [b[i] for b in rights], component) for i in range(2)
     ]
+
+
+def two_at_a_time(start, stop, one_row):
+    def two_rows(i, carry):
+        for n in range(2):
+            one_row(start + 2 * i + n, carry)
+        return carry
+
+    lax.fori_loop(0, (stop - start) // 2, two_rows, 0)
 
 
 def sources(cells, cotangent):
@@ -229,8 +243,8 @@
             def one_level(z, inner_carry):
                 for c in both:
                     copy_of(
-                        below_above.at[3], shared.at[level * groups + group], shared_send.at[z],
-                        shared_recv.at[level], x * inner + z * 2 + c, wedge,
+                        below_above.at[3], shared.at[level * groups + group], shared_send,
+                        shared_recv, x * inner + z * 2 + c, wedge,
                     ).start()
                 return inner_carry
 
@@ -242,7 +256,7 @@
         def one_level(z, carry):
             for c in both:
                 copy_of(
-                    below_above.at[3], along.at[level], along_send.at[z], along_recv.at[level],
+                    below_above.at[3], along.at[level], along_send, along_recv,
                     group * inner + z * 2 + c, wedge,
                 ).start()
             return carry
@@ -298,7 +312,7 @@
     def halo_copies(number, high_rows, low_rows, packed, radial_halo, phi_halo):
         def copy(which, source, target, peer):
             return pltpu.make_async_remote_copy(
-                src_ref=source, dst_ref=target, send_sem=halo_send.at[4 * number + which],
+                src_ref=source, dst_ref=target, send_sem=halo_send.at[which],
                 recv_sem=halo_recv.at[4 * number + which], device_id=peer, device_id_type=MESH,
             )
 
@@ -354,19 +368,15 @@
     def keep(direction, side, where, state):
         for n, k in enumerate(STEADY):
             prep[direction, side, n, where, :] = state[k]
-        prep[direction, side, len(STEADY), where, :] = 1.0 / jnp.maximum(
-            state[0], MINIMUM_DENSITY
-        )
-        prep[direction, side, len(STEADY) + 1, where, :] = (
-            state[2] * state[2] + state[3] * state[3]
-        )
+        for n, value in enumerate(side_ready(state)):
+            prep[direction, side, len(STEADY) + n, where, :] = value
 
     def kept(direction, where, left, right):
         ready = []
         for side, state in enumerate((left, right)):
             for n, k in enumerate(STEADY):
                 state[k] = prep[direction, side, n, where, :]
-            ready.append(tuple(prep[direction, side, len(STEADY) + n, where, :] for n in (0, 1)))
+            ready.append(tuple(prep[direction, side, len(STEADY) + n, where, :] for n in range(3)))
         return ready
 
     def prepare(u):
@@ -424,12 +434,13 @@
             scale = tab[0, pl.ds(r, 1), :]
             cells = [u[k, pl.ds(pl.multiple_of(8 + r * width, 8), width), :] for k in range(NV)]
             source = sources(cells, cotangent)
+            across = scale * inverse_sine
             for k in range(NV):
                 through = th[k, store, :]
-                change = (pltpu.roll(through, 1, 1) - through) * inverse_sine
+                value = cells[k] + across * (pltpu.roll(through, 1, 1) - through)
                 if source[k] is not None:
-                    change = change + source[k]
-                acc[k, store, :] = cells[k] + scale * change
+                    value = value + scale * source[k]
+                acc[k, store, :] = value
 
         def second(i, n):
             r = jnp.clip((i - 1) * together, 0, rows - together) + n
@@ -441,9 +452,9 @@
                 cell = u[k, pl.ds(pl.multiple_of(8 + r * width, 8), width), :]
                 right[k] = jnp.where(wide_lane == 127, cell, pltpu.roll(value, 127, 1))
             ready = kept(0, store, left, right) if prepared else (None, None)
-            flux = twice_flux(left, right, 2, ready)
+            flux = twice_flux(left, right, 2, ready, sine)
             for k in range(NV):
-                th[k, store, :] = flux[k] * sine
+                th[k, store, :] = flux[k]
 
         def first(i, n):
             r = jnp.minimum(i * together, rows - together) + n
@@ -508,7 +519,7 @@
                 fr[k, pl.ds(store, width), :] = flux[k]
             return carry
 
-        lax.fori_loop(1, rows - 1, one_row, 0)
+        two_at_a_time(1, rows - 1, one_row)
 
     def edge_azimuth(u, halo):
         for side in range(2):
@@ -597,11 +608,12 @@
         return carry
 
     with jax.named_scope("final1"):
-        lax.fori_loop(0, rows, section_one_row, 0)
-    pack(u1, pk1)
+        two_at_a_time(0, rows, section_one_row)
     for k in range(NV):
         sr[0, k] = u1[k, pl.ds(8 + (rows - 2) * width, 2 * width), :]
         sr[1, k] = u1[k, pl.ds(8, 2 * width), :]
+    pack(u1, pk1)
+    wait_sent(first_halos)
     second_halos = halo_copies(1, sr.at[0], sr.at[1], pk1, hr1, hp1)
     start_halos(
         second_halos, hr1,
@@ -618,15 +630,11 @@
 
             @pl.when(group == x)
             def _(count=x):
-                def one_level(z, value):
-                    many(count, shared_send.at[0], shared_recv.at[z]).wait_recv()
-                    for n in range(count):
-                        value = value + shared[z * groups + n]
-                    return value
-
-                inside_rows[0] = lax.fori_loop(
-                    0, levels, one_level, jnp.zeros((1, 128), jnp.float32)
-                )
+                many(count * levels, shared_send, shared_recv).wait_recv()
+                value = [shared[n] for n in range(count)]
+                for z in range(1, levels):
+                    value = [value[n] + shared[z * groups + n] for n in range(count)]
+                inside_rows[0] = functools.reduce(jnp.add, value)
                 for passer, z_start, z_stop in passers:
 
                     @pl.when(jnp.logical_and(sender, level == passer))
@@ -636,11 +644,12 @@
                                 pass_copy(z, c).start()
 
     def gather_along():
-        def one_level(z, value):
-            many(1, along_send.at[0], along_recv.at[z]).wait_recv()
-            return value + along[z]
-
-        return lax.fori_loop(0, level, one_level, jnp.zeros((1, 128), jnp.float32))
+        for z in range(1, levels):
+
+            @pl.when(level == z)
+            def _(z=z):
+                many(z, along_send, along_recv).wait_recv()
+                inside_rows[2] = functools.reduce(jnp.add, [along[n] for n in range(z)])
 
     half_of = lambda index: jnp.where(lane < index, 1.0, jnp.where(lane == index, 0.5, 0.0))
     none = jnp.zeros((8, 128), jnp.float32)
@@ -663,7 +672,7 @@
         prepare(u1)
     with jax.named_scope("m1_wait"):
         pl.when(is_near)(gather_across)
-        inside = gather_along()
+        gather_along()
         pl.when(jnp.logical_and(group > 0, jnp.logical_not(is_near)))(
             lambda: pass_copy(levels - 1, 1).wait_recv()
         )
@@ -671,6 +680,7 @@
         pl.when(place < last)(lambda: side_copy(1).wait_recv())
     below, above, own = below_above[0], below_above[1], below_above[2]
     smaller_x = jnp.where(is_near, inside_rows[0], inside_rows[1])
+    inside = jnp.where(level > 0, inside_rows[2], 0.0)
     inside = inside + jnp.where(group > 0, smaller_x, 0.0) + jnp.where(core_index == 1, below, 0.0)
     table = (
         inside + weights[0] * own,
@@ -692,7 +702,7 @@
         return carry
 
     with jax.named_scope("grav"):
-        lax.fori_loop(0, rows, gravity_row, 0)
+        two_at_a_time(0, rows, gravity_row)
 
     with jax.named_scope("pre2"):
         polar_and_azimuth(u1, prepared=True)
@@ -736,22 +746,22 @@
         return carry
 
     with jax.named_scope("final2"):
-        lax.fori_loop(0, rows, section_two_row, 0)
+        two_at_a_time(0, rows, section_two_row)
     with jax.named_scope("drain"):
         @pl.when(sender)
         def _():
             for x in range(groups - 1):
 
                 @pl.when(group == x)
-                def _(count=2 * (groups - 1 - x)):
-                    for z in range(near):
-                        many(count, shared_send.at[z], shared_recv.at[0]).wait_send()
-
-            def sent_along(z, carry):
-                many(2, along_send.at[z], along_recv.at[0]).wait_send()
-                return carry
-
-            lax.fori_loop(level + 1, levels, sent_along, 0)
+                def _(count=2 * near * (groups - 1 - x)):
+                    many(count, shared_send, shared_recv).wait_send()
+
+            for z in range(levels - 1):
+                pl.when(level == z)(
+                    lambda count=2 * (levels - 1 - z): many(
+                        count, along_send, along_recv
+                    ).wait_send()
+                )
             for passer, z_start, z_stop in passers:
                 pl.when(jnp.logical_and(group > 0, level == passer))(
                     lambda count=2 * (z_stop - z_start): many(
@@ -763,14 +773,14 @@
         wedge_all().wait_send()
         pl.when(place < last)(lambda: side_copy(0).wait_send())
         pl.when(place > 0)(lambda: side_copy(1).wait_send())
-        wait_sent(first_halos)
         wait_sent(second_halos)
 
 
 def put_out(advanced, enclosed, advanced_hbm, enclosed_hbm, sem):
     copies = [
-        pltpu.make_async_copy(advanced.at[k], advanced_hbm.at[k], sem.at[k]) for k in range(NV)
-    ] + [pltpu.make_async_copy(enclosed, enclosed_hbm, sem.at[NV])]
+        pltpu.make_async_copy(advanced, advanced_hbm, sem.at[0]),
+        pltpu.make_async_copy(enclosed, enclosed_hbm, sem.at[1]),
+    ]
     for copy in copies:
         copy.start()
     for copy in copies:
@@ -824,12 +834,11 @@
             vmem(NV, cells + width, lanes),
             vmem(NV, cells, lanes),
             vmem(NV, cells, lanes), vmem(NV, cells, lanes), vmem(NV, cells, lanes),
-            vmem(3, 2, len(STEADY) + 2, cells, lanes),
+            vmem(3, 2, len(STEADY) + 3, cells, lanes),
             vmem(slabs // 2, 1, lanes), vmem(inner // 2, 1, lanes), vmem(4, 1, lanes), vmem(wedges, 1, lanes),
-            vmem(wedges, 1, lanes), vmem(2, 1, lanes), vmem(6, 8, lanes),
+            vmem(wedges, 1, lanes), vmem(3, 1, lanes), vmem(6, 8, lanes),
             vmem(3, 8, lanes), vmem(16, lanes), vmem(8, lanes), pltpu.SMEM((1,), f32),
-            dma(4), dma(8), dma(8), dma(inner // 8), dma(inner // 2),
-            dma(inner // 2), dma(inner // 2), dma(2), dma(2),
+            dma(4), dma(4), dma(8), *[pltpu.SemaphoreType.DMA] * 4, dma(2), dma(2),
             pltpu.SemaphoreType.DMA, pltpu.SemaphoreType.DMA,
             pltpu.SemaphoreType.DMA, pltpu.SemaphoreType.DMA,
             pltpu.SemaphoreType.DMA, pltpu.SemaphoreType.DMA,
@@ -847,7 +856,7 @@
         ),
         in_specs=[pl.BlockSpec(memory_space=pltpu.VMEM)] * 2,
         out_specs=[pl.BlockSpec(memory_space=pltpu.HBM)] * 2,
-        scratch_shapes=[dma(NV + 1)],
+        scratch_shapes=[dma(2)],
         compiler_params=pltpu.CompilerParams(vmem_limit_bytes=4 << 20),
     )(advanced, enclosed)
     return advanced.reshape(conserved.shape), enclosed.reshape(rows)

time: 19.7 us -> 19.2 us (0.975)
  Pallas kernels: 18.3 us -> 17.8 us
    pallas_call x1, Pallas kernels: 17.4 us -> 17 us  [body(): pl.pallas_call(functools.partial(kernel, sizes), out_shape=(jax.ShapeDtyp...]
where the time goes in v6:
time: 19.2 us; the launch traced here: 19.1 us
  Pallas kernels  17.8 us (93%)
  between operations  1.28 us (7%)
    pallas_call x1, Pallas kernels, body(): pl.pallas_call(functools.partial(kernel, sizes), out_shape=(jax.ShapeDtyp...  17 us
    pallas_call x1, Pallas kernels, body(): pl.pallas_call(put_out, out_shape=(jax.ShapeDtypeStruct((NV, cells, lanes...  0.81 us

profile of v6, /device:TPU:7, one launch (start us, length us, event | category | flops | bytes accessed | tf_op | source)
XLA Modules:
  0.0 19.1 jit_solution(10106598373958583323)
XLA Ops:
  1.3 17.0 %shard_map.50 = (f32[8,128,128]{2,1,0:T(8,128)S(1)}, f32[1,8]{1,0:T(1,128)S(1)}) custom-call(f32[8,128,128]{2,1,0:T(8,128)} %bitcast.3, f32[1]{0:T(128)S(6)} %copy.5.mass_hbm, f32[8,128]{1,0:T(8,128)} %constant.2.clone.angles_hbm), custom_call_target="tpu_custom_call" | custom-call | tf_op jit(solution)/shard_map/pallas_call | solution.py:811
  18.2 0.8 %shard_map.51 = (f32[8,128,128]{2,1,0:T(8,128)}, f32[1,8]{1,0:T(1,128)}) custom-call(f32[8,128,128]{2,1,0:T(8,128)S(1)} %get-tuple-element.6.advanced, f32[1,8]{1,0:T(1,128)S(1)} %get-tuple-element.7.enclosed), custom_call_target="tpu_custom_call" | custom-call | tf_op jit(solution)/shard_map/pallas_call | solution.py:851

commit v7 on v6

--- a/solution.py
+++ b/solution.py
@@ -89,6 +89,21 @@
     lax.fori_loop(0, (stop - start) // 2, two_rows, 0)
 
 
+def row_sum(r, part, width, acc, fp, fr, tab, ct):
+    store = r * width if isinstance(r, int) else pl.multiple_of(r * width, 8)
+    below = r * (width + 8) if isinstance(r, int) else pl.multiple_of(r * (width + 8), 8)
+    following = store + width if isinstance(r, int) else pl.multiple_of(store + width, 8)
+    low_area, high_area = part * tab[1, pl.ds(r, 1), :], part * tab[2, pl.ds(r, 1), :]
+    across = part * tab[0, pl.ds(r, 1), :] * ct[6:7, :]
+    return [
+        acc[k, pl.ds(store, width), :]
+        + across * (fp[k, pl.ds(below, width), :] - fp[k, pl.ds(below + 1, width), :])
+        + low_area * fr[k, pl.ds(store, width), :]
+        - high_area * fr[k, pl.ds(following, width), :]
+        for k in range(NV)
+    ]
+
+
 def sources(cells, cotangent):
     density = jnp.maximum(cells[0], MINIMUM_DENSITY)
     inverse = 1.0 / density
@@ -102,14 +117,14 @@
     source[1] = 2.0 * pressure + (cells[2] * speed[2] + spin)
     source[2] = (pressure + spin) * cotangent - cells[1] * speed[2]
     source[3] = -speed[3] * (cells[1] + cells[2] * cotangent)
-    return source
+    return source, density
 
 
 def kernel(
     sizes, state_hbm, mass_hbm, angles_hbm,
-    outv, enclosed_ref,
-    u0, u1, hr0, hr1, hp0, hp1, pk0, pk1, sr, acc, fp, fr, sl, lt, rt, th, prep,
-    shared, along, below_above, wedge_rows, chip_rows, inside_rows, weights, tab, grav, ct, core,
+    acc, fp, fr, tab, ct, enclosed_ref,
+    u0, u1, hr0, hr1, hp0, hp1, pk0, pk1, sr, sl, lt, rt, th, prep,
+    shared, along, below_above, wedge_rows, chip_rows, inside_rows, weights, grav, core,
     in_sem, halo_send, halo_recv, shared_send, shared_recv, along_send, along_recv,
     side_send, side_recv, pass_send, pass_recv, wedge_send, wedge_recv, chip_send, chip_recv,
     from_near, from_far,
@@ -220,7 +235,6 @@
         radius * radius * (radial_step * theta_step * phi_step)
     )
     wedge_rows[0] = jnp.sum(jnp.where(lane == row, shells, 0.0), axis=0, keepdims=True)
-    fetch.wait()
 
     def pack(source, packed):
         for side, zones in enumerate(((width - 2, width - 1), (0, 1))):
@@ -228,7 +242,6 @@
                 for i, zone in enumerate(zones):
                     packed[side, k, i] = source[k, pl.ds(8 + zone, 8, stride=width), :]
 
-    pack(u0, pk0)
     with jax.named_scope("barrier_wait"):
         pl.semaphore_wait(barrier, greetings)
 
@@ -308,6 +321,9 @@
 
     for step in range(1, wedges):
         wedge_copy(step).start()
+
+    fetch.wait()
+    pack(u0, pk0)
 
     def halo_copies(number, high_rows, low_rows, packed, radial_halo, phi_halo):
         def copy(which, source, target, peer):
@@ -433,13 +449,21 @@
             store = pl.ds(pl.multiple_of(r * width, 8), width)
             scale = tab[0, pl.ds(r, 1), :]
             cells = [u[k, pl.ds(pl.multiple_of(8 + r * width, 8), width), :] for k in range(NV)]
-            source = sources(cells, cotangent)
+            source, density = sources(cells, cotangent)
+            pull = grav[pl.ds(r, 1), :]
             across = scale * inverse_sine
             for k in range(NV):
                 through = th[k, store, :]
                 value = cells[k] + across * (pltpu.roll(through, 1, 1) - through)
                 if source[k] is not None:
                     value = value + scale * source[k]
+                if prepared:
+                    if k == 1:
+                        value = value - pull * density
+                    elif k == 4:
+                        value = value - pull * cells[1]
+                    before = u0[k, pl.ds(pl.multiple_of(8 + r * width, 8), width), :]
+                    value = 0.5 * (before + value)
                 acc[k, store, :] = value
 
         def second(i, n):
@@ -549,22 +573,8 @@
                 for k in range(NV):
                     fr[k, pl.ds(face * width, width), :] = flux[k]
 
-    azimuth_scale = 0.5 / phi_step
-
     def advanced_row(r):
-        store = pl.multiple_of(r * width, 8)
-        low_area, high_area = tab[1, pl.ds(r, 1), :], tab[2, pl.ds(r, 1), :]
-        across = tab[0, pl.ds(r, 1), :] * ct[1:2, :] * azimuth_scale
-        below = pl.multiple_of(r * span, 8)
-        values = []
-        for k in range(NV):
-            values.append(
-                acc[k, pl.ds(store, width), :]
-                + across * (fp[k, pl.ds(below, width), :] - fp[k, pl.ds(below + 1, width), :])
-                + low_area * fr[k, pl.ds(store, width), :]
-                - high_area * fr[k, pl.ds(pl.multiple_of(store + width, 8), width), :]
-            )
-        return values
+        return row_sum(r, 1.0, width, acc, fp, fr, tab, ct)
 
     with jax.named_scope("pre1"):
         polar_and_azimuth(u0)
@@ -733,20 +743,6 @@
     with jax.named_scope("edge_rad2"):
         edge_radial(u1, hr1)
 
-    def section_two_row(r, carry):
-        values = advanced_row(r)
-        base = pl.ds(pl.multiple_of(8 + r * width, 8), width)
-        pull = grav[pl.ds(r, 1), :]
-        values[1] = values[1] - pull * jnp.maximum(u1[0, base, :], MINIMUM_DENSITY)
-        values[4] = values[4] - pull * u1[1, base, :]
-        for k in range(NV):
-            outv[k, pl.ds(pl.multiple_of(r * width, 8), width), :] = 0.5 * (
-                u0[k, base, :] + values[k]
-            )
-        return carry
-
-    with jax.named_scope("final2"):
-        two_at_a_time(0, rows, section_two_row)
     with jax.named_scope("drain"):
         @pl.when(sender)
         def _():
@@ -776,13 +772,22 @@
         wait_sent(second_halos)
 
 
-def put_out(advanced, enclosed, advanced_hbm, enclosed_hbm, sem):
-    copies = [
-        pltpu.make_async_copy(advanced, advanced_hbm, sem.at[0]),
-        pltpu.make_async_copy(enclosed, enclosed_hbm, sem.at[1]),
-    ]
-    for copy in copies:
-        copy.start()
+def put_out(
+    rows, width, acc, fp, fr, tab, ct, enclosed, advanced_hbm, enclosed_hbm, outv, sem
+):
+    copies = [pltpu.make_async_copy(enclosed, enclosed_hbm, sem.at[rows // 2])]
+    copies[0].start()
+    for pair in range(rows // 2):
+        for r in (2 * pair, 2 * pair + 1):
+            for k, value in enumerate(row_sum(r, 0.5, width, acc, fp, fr, tab, ct)):
+                outv[k, r * width : (r + 1) * width, :] = value
+        where = pl.ds(2 * pair * width, 2 * width)
+        copies.append(
+            pltpu.make_async_copy(
+                outv.at[:, where, :], advanced_hbm.at[:, where, :], sem.at[pair]
+            )
+        )
+        copies[-1].start()
     for copy in copies:
         copy.wait()
 
@@ -800,6 +805,7 @@
     angles[2] = np.cos(centers) / np.sin(centers)
     angles[3] = np.sin(centers)
     angles[4] = np.where(np.arange(lanes) == lanes - 1, 0.0, 0.5)
+    angles[6] = angles[1] * (0.5 / phi_step)
     angles[5] = np.where(np.arange(lanes) == 0, 0.0, 0.5)
     angles = jnp.asarray(angles.astype(np.float32))
     sizes = (rows, width, slabs, wedges, groups, radial_step, theta_step, phi_step, timestep)
@@ -808,21 +814,25 @@
     dma = lambda count: pltpu.SemaphoreType.DMA((count,))
     in_hbm = lambda value: pltpu.with_memory_space_constraint(value, pltpu.HBM)
     cells = rows * width
-    advanced, enclosed = pl.pallas_call(
+    *parts, enclosed = pl.pallas_call(
         functools.partial(kernel, sizes),
-        out_shape=(
-            jax.ShapeDtypeStruct((NV, cells, lanes), f32),
-            jax.ShapeDtypeStruct((1, rows), f32),
-        ),
+        out_shape=[
+            jax.ShapeDtypeStruct(shape, f32)
+            for shape in (
+                (NV, cells, lanes),
+                (NV, rows * (width + 8), lanes),
+                (NV, cells + width, lanes),
+                (3, 8, lanes),
+                (8, lanes),
+                (1, rows),
+            )
+        ],
         in_specs=[
             pl.BlockSpec(memory_space=pltpu.HBM),
             pl.BlockSpec(memory_space=pltpu.HBM),
             pl.BlockSpec(memory_space=pltpu.HBM),
         ],
-        out_specs=(
-            pl.BlockSpec(memory_space=pltpu.VMEM),
-            pl.BlockSpec(memory_space=pltpu.VMEM),
-        ),
+        out_specs=[pl.BlockSpec(memory_space=pltpu.VMEM)] * 6,
         scratch_shapes=[
             vmem(NV, cells + 16, lanes), vmem(NV, cells + 16, lanes),
             vmem(2, NV, 2 * width, lanes), vmem(2, NV, 2 * width, lanes),
@@ -830,14 +840,11 @@
             vmem(2, NV, 2, 8, lanes), vmem(2, NV, 2, 8, lanes),
             vmem(2, NV, 2 * width, lanes),
             vmem(NV, cells, lanes),
-            vmem(NV, rows * (width + 8), lanes),
-            vmem(NV, cells + width, lanes),
-            vmem(NV, cells, lanes),
             vmem(NV, cells, lanes), vmem(NV, cells, lanes), vmem(NV, cells, lanes),
             vmem(3, 2, len(STEADY) + 3, cells, lanes),
             vmem(slabs // 2, 1, lanes), vmem(inner // 2, 1, lanes), vmem(4, 1, lanes), vmem(wedges, 1, lanes),
             vmem(wedges, 1, lanes), vmem(3, 1, lanes), vmem(6, 8, lanes),
-            vmem(3, 8, lanes), vmem(16, lanes), vmem(8, lanes), pltpu.SMEM((1,), f32),
+            vmem(16, lanes), pltpu.SMEM((1,), f32),
             dma(4), dma(4), dma(8), *[pltpu.SemaphoreType.DMA] * 4, dma(2), dma(2),
             pltpu.SemaphoreType.DMA, pltpu.SemaphoreType.DMA,
             pltpu.SemaphoreType.DMA, pltpu.SemaphoreType.DMA,
@@ -849,16 +856,16 @@
         ),
     )(in_hbm(conserved.reshape(NV, cells, lanes)), core_mass, in_hbm(angles))
     advanced, enclosed = pl.pallas_call(
-        put_out,
+        functools.partial(put_out, rows, width),
         out_shape=(
             jax.ShapeDtypeStruct((NV, cells, lanes), f32),
             jax.ShapeDtypeStruct((1, rows), f32),
         ),
-        in_specs=[pl.BlockSpec(memory_space=pltpu.VMEM)] * 2,
+        in_specs=[pl.BlockSpec(memory_space=pltpu.VMEM)] * 6,
         out_specs=[pl.BlockSpec(memory_space=pltpu.HBM)] * 2,
-        scratch_shapes=[dma(2)],
-        compiler_params=pltpu.CompilerParams(vmem_limit_bytes=4 << 20),
-    )(advanced, enclosed)
+        scratch_shapes=[vmem(NV, cells, lanes), dma(rows // 2 + 1)],
+        compiler_params=pltpu.CompilerParams(vmem_limit_bytes=8 << 20),
+    )(*parts, enclosed)
     return advanced.reshape(conserved.shape), enclosed.reshape(rows)
 
 

time: 19.2 us -> 19 us (0.990)
  Pallas kernels: 17.8 us -> 17.6 us
where the time goes in v7:
time: 19 us; the launch traced here: 18.9 us
  Pallas kernels  17.6 us (93%)
  between operations  1.28 us (7%)
    pallas_call x1, Pallas kernels, body(): pl.pallas_call(functools.partial(kernel, sizes), out_shape=[jax.ShapeDtyp...  16.8 us
    pallas_call x1, Pallas kernels, body(): pl.pallas_call(functools.partial(put_out, rows, width), out_shape=(jax.Sh...  0.87 us

profile of v7, /device:TPU:7, one launch (start us, length us, event | category | flops | bytes accessed | tf_op | source)
XLA Modules:
  0.0 18.9 jit_solution(12322223744601300408)
XLA Ops:
  1.3 16.8 %shard_map.50 = (f32[8,128,128]{2,1,0:T(8,128)S(1)}, f32[8,192,128]{2,1,0:T(8,128)S(1)}, f32[8,144,128]{2,1,0:T(8,128)S(1)}, f32[3,8,128]{2,1,0:T(8,128)S(1)}, f32[8,128]{1,0:T(8,128)S(1)}, /*index=5*/f32[1,8]{1,0:T(1,128)S(1)}) custom-call(f32[8,128,128]{2,1,0:T(8,128)} %bitcast.3, f32[1]{0:T(128)S(6)} %copy.5.mass_hbm, f32[8,128]{1,0:T(8,128)} %constant.2.clone.angles_hbm), custom_call_target="tpu_custom_call" | custom-call | tf_op jit(solution)/shard_map/pallas_call | solution.py:817
  18.0 0.9 %shard_map.51 = (f32[8,128,128]{2,1,0:T(8,128)}, f32[1,8]{1,0:T(1,128)}) custom-call(f32[8,128,128]{2,1,0:T(8,128)S(1)} %get-tuple-element.10.acc, f32[8,192,128]{2,1,0:T(8,128)S(1)} %get-tuple-element.11.fp, f32[8,144,128]{2,1,0:T(8,128)S(1)} %get-tuple-element.12.fr, f32[3,8,128]{2,1,0:T(8,128)S(1)} %get-tuple-element.13.tab, ...), custom_call_target="tpu_custom_call" | custom-call | tf_op jit(solution)/shard_map/pallas_call | solution.py:858

commit v8 on v7

--- a/solution.py
+++ b/solution.py
@@ -438,8 +438,35 @@
 
         lax.fori_loop(1, rows - 1, one_inner_row, 0)
 
+    def inner_radial_row(u, prepared=False):
+        moving = MOVED if prepared else range(NV)
+
+        def one_row(r, carry=0):
+            base = pl.multiple_of(8 + r * width, 8)
+            store = pl.multiple_of(r * width, 8)
+            left, right = {}, {}
+            for k in moving:
+                cell = u[k, pl.ds(base, width), :]
+                low = 0.5 * (cell - u[k, pl.ds(base - width, width), :])
+                high = 0.5 * (u[k, pl.ds(base + width, width), :] - cell)
+                slope = half_slope(low, high)
+                right[k] = cell - slope
+                left[k] = sl[k, pl.ds(store - width, width), :]
+                sl[k, pl.ds(store, width), :] = cell + slope
+            ready = kept(2, pl.ds(store, width), left, right) if prepared else (None, None)
+            flux = twice_flux(left, right, 1, ready)
+            for k in range(NV):
+                fr[k, pl.ds(store, width), :] = flux[k]
+            return carry
+
+        return one_row
+
+    def inner_radial(u):
+        two_at_a_time(1, rows - 1, inner_radial_row(u))
+
     def polar_and_azimuth(u, prepared=False):
         moving = MOVED if prepared else range(NV)
+        radial_row = inner_radial_row(u, prepared)
 
         together = 2 if prepared else 1
         sine, inverse_sine, cotangent, mask = ct[0:1, :], ct[1:2, :], ct[2:3, :], ct[4:5, :]
@@ -514,36 +541,20 @@
 
         steps = rows // together
         if prepared:
+            third_part = (rows - 2) // 3
             run(0, (first,))
+            for r in range(1, 1 + third_part):
+                radial_row(jnp.int32(r))
             run(1, (second, first))
             lax.fori_loop(2, steps, one_step, 0)
             run(steps, (third, second))
+            for r in range(1 + third_part, 1 + 2 * third_part):
+                radial_row(jnp.int32(r))
             run(steps + 1, (third,))
+            for r in range(1 + 2 * third_part, rows - 1):
+                radial_row(jnp.int32(r))
         else:
             lax.fori_loop(0, steps + 2, one_step, 0)
-
-    def inner_radial(u, prepared=False):
-        moving = MOVED if prepared else range(NV)
-
-        def one_row(r, carry):
-            base = pl.multiple_of(8 + r * width, 8)
-            store = pl.multiple_of(r * width, 8)
-            left, right = {}, {}
-            for k in moving:
-                cell = u[k, pl.ds(base, width), :]
-                low = 0.5 * (cell - u[k, pl.ds(base - width, width), :])
-                high = 0.5 * (u[k, pl.ds(base + width, width), :] - cell)
-                slope = half_slope(low, high)
-                right[k] = cell - slope
-                left[k] = sl[k, pl.ds(store - width, width), :]
-                sl[k, pl.ds(store, width), :] = cell + slope
-            ready = kept(2, pl.ds(store, width), left, right) if prepared else (None, None)
-            flux = twice_flux(left, right, 1, ready)
-            for k in range(NV):
-                fr[k, pl.ds(store, width), :] = flux[k]
-            return carry
-
-        two_at_a_time(1, rows - 1, one_row)
 
     def edge_azimuth(u, halo):
         for side in range(2):
@@ -716,8 +727,6 @@
 
     with jax.named_scope("pre2"):
         polar_and_azimuth(u1, prepared=True)
-    with jax.named_scope("rad2"):
-        inner_radial(u1, prepared=True)
     with jax.named_scope("h2_phi_wait"):
         second_halos[2].wait_recv()
         second_halos[3].wait_recv()

time: 19 us -> 18.9 us (level)
  no operation moved by 1% of the time
where the time goes in v8:
time: 18.9 us; the launch traced here: 18.8 us
  Pallas kernels  17.5 us (93%)
  between operations  1.28 us (7%)
    pallas_call x1, Pallas kernels, body(): pl.pallas_call(functools.partial(kernel, sizes), out_shape=[jax.ShapeDtyp...  16.7 us
    pallas_call x1, Pallas kernels, body(): pl.pallas_call(functools.partial(put_out, rows, width), out_shape=(jax.Sh...  0.87 us

profile of v8, /device:TPU:7, one launch (start us, length us, event | category | flops | bytes accessed | tf_op | source)
XLA Modules:
  0.0 18.8 jit_solution(11891717299017560188)
XLA Ops:
  1.3 16.7 %shard_map.50 = (f32[8,128,128]{2,1,0:T(8,128)S(1)}, f32[8,192,128]{2,1,0:T(8,128)S(1)}, f32[8,144,128]{2,1,0:T(8,128)S(1)}, f32[3,8,128]{2,1,0:T(8,128)S(1)}, f32[8,128]{1,0:T(8,128)S(1)}, /*index=5*/f32[1,8]{1,0:T(1,128)S(1)}) custom-call(f32[8,128,128]{2,1,0:T(8,128)} %bitcast.3, f32[1]{0:T(128)S(6)} %copy.5.mass_hbm, f32[8,128]{1,0:T(8,128)} %constant.2.clone.angles_hbm), custom_call_target="tpu_custom_call" | custom-call | tf_op jit(solution)/shard_map/pallas_call | solution.py:826
  17.9 0.9 %shard_map.51 = (f32[8,128,128]{2,1,0:T(8,128)}, f32[1,8]{1,0:T(1,128)}) custom-call(f32[8,128,128]{2,1,0:T(8,128)S(1)} %get-tuple-element.10.acc, f32[8,192,128]{2,1,0:T(8,128)S(1)} %get-tuple-element.11.fp, f32[8,144,128]{2,1,0:T(8,128)S(1)} %get-tuple-element.12.fr, f32[3,8,128]{2,1,0:T(8,128)S(1)} %get-tuple-element.13.tab, ...), custom_call_target="tpu_custom_call" | custom-call | tf_op jit(solution)/shard_map/pallas_call | solution.py:867

commit v9 on v8

--- a/solution.py
+++ b/solution.py
@@ -464,7 +464,7 @@
     def inner_radial(u):
         two_at_a_time(1, rows - 1, inner_radial_row(u))
 
-    def polar_and_azimuth(u, prepared=False):
+    def polar_and_azimuth(u, prepared=None):
         moving = MOVED if prepared else range(NV)
         radial_row = inner_radial_row(u, prepared)
 
@@ -550,9 +550,12 @@
             run(steps, (third, second))
             for r in range(1 + third_part, 1 + 2 * third_part):
                 radial_row(jnp.int32(r))
-            run(steps + 1, (third,))
             for r in range(1 + 2 * third_part, rows - 1):
                 radial_row(jnp.int32(r))
+            prepared()
+            run(steps + 1, (third,))
+            edge_azimuth(u1, hp1)
+            edge_radial(u1, hr1)
         else:
             lax.fori_loop(0, steps + 2, one_step, 0)
 
@@ -725,33 +728,28 @@
     with jax.named_scope("grav"):
         two_at_a_time(0, rows, gravity_row)
 
-    with jax.named_scope("pre2"):
-        polar_and_azimuth(u1, prepared=True)
-    with jax.named_scope("h2_phi_wait"):
+    def outer_faces():
         second_halos[2].wait_recv()
         second_halos[3].wait_recv()
-    pull = grav[0:8, :]
-    for side in range(2):
-        for i in range(2):
-            hp1[side, 1, i] = hp1[side, 1, i] - pull * jnp.maximum(
-                hp0[side, 0, i], MINIMUM_DENSITY
-            )
-            hp1[side, 4, i] = hp1[side, 4, i] - pull * hp0[side, 1, i]
-    with jax.named_scope("edge_phi2"):
-        edge_azimuth(u1, hp1)
-    with jax.named_scope("h2_rad_wait"):
         wait_radial(second_halos)
-    for side in range(2):
-        for i in range(2):
-            which = pl.ds(width * i, width)
-            pull = grav[8 + 2 * side + i : 9 + 2 * side + i, :]
-            hr1[side, 1, which, :] = hr1[side, 1, which, :] - pull * jnp.maximum(
-                hr0[side, 0, which, :], MINIMUM_DENSITY
-            )
-            hr1[side, 4, which, :] = hr1[side, 4, which, :] - pull * hr0[side, 1, which, :]
-    with jax.named_scope("edge_rad2"):
-        edge_radial(u1, hr1)
-
+        pull = grav[0:8, :]
+        for side in range(2):
+            for i in range(2):
+                hp1[side, 1, i] = hp1[side, 1, i] - pull * jnp.maximum(
+                    hp0[side, 0, i], MINIMUM_DENSITY
+                )
+                hp1[side, 4, i] = hp1[side, 4, i] - pull * hp0[side, 1, i]
+        for side in range(2):
+            for i in range(2):
+                which = pl.ds(width * i, width)
+                pull = grav[8 + 2 * side + i : 9 + 2 * side + i, :]
+                hr1[side, 1, which, :] = hr1[side, 1, which, :] - pull * jnp.maximum(
+                    hr0[side, 0, which, :], MINIMUM_DENSITY
+                )
+                hr1[side, 4, which, :] = hr1[side, 4, which, :] - pull * hr0[side, 1, which, :]
+
+    with jax.named_scope("pre2"):
+        polar_and_azimuth(u1, outer_faces)
     with jax.named_scope("drain"):
         @pl.when(sender)
         def _():

time: 18.9 us -> 18.9 us (level)
  no operation moved by 1% of the time
where the time goes in v9:
time: 18.9 us; the launch traced here: 18.8 us
  Pallas kernels  17.5 us (93%)
  between operations  1.28 us (7%)
    pallas_call x1, Pallas kernels, body(): pl.pallas_call(functools.partial(kernel, sizes), out_shape=[jax.ShapeDtyp...  16.6 us
    pallas_call x1, Pallas kernels, body(): pl.pallas_call(functools.partial(put_out, rows, width), out_shape=(jax.Sh...  0.87 us

profile of v9, /device:TPU:7, one launch (start us, length us, event | category | flops | bytes accessed | tf_op | source)
XLA Modules:
  0.0 18.8 jit_solution(12344320222411836288)
XLA Ops:
  1.3 16.6 %shard_map.50 = (f32[8,128,128]{2,1,0:T(8,128)S(1)}, f32[8,192,128]{2,1,0:T(8,128)S(1)}, f32[8,144,128]{2,1,0:T(8,128)S(1)}, f32[3,8,128]{2,1,0:T(8,128)S(1)}, f32[8,128]{1,0:T(8,128)S(1)}, /*index=5*/f32[1,8]{1,0:T(1,128)S(1)}) custom-call(f32[8,128,128]{2,1,0:T(8,128)} %bitcast.3, f32[1]{0:T(128)S(6)} %copy.5.mass_hbm, f32[8,128]{1,0:T(8,128)} %constant.2.clone.angles_hbm), custom_call_target="tpu_custom_call" | custom-call | tf_op jit(solution)/shard_map/pallas_call | solution.py:824
  17.9 0.9 %shard_map.51 = (f32[8,128,128]{2,1,0:T(8,128)}, f32[1,8]{1,0:T(1,128)}) custom-call(f32[8,128,128]{2,1,0:T(8,128)S(1)} %get-tuple-element.10.acc, f32[8,192,128]{2,1,0:T(8,128)S(1)} %get-tuple-element.11.fp, f32[8,144,128]{2,1,0:T(8,128)S(1)} %get-tuple-element.12.fr, f32[3,8,128]{2,1,0:T(8,128)S(1)} %get-tuple-element.13.tab, ...), custom_call_target="tpu_custom_call" | custom-call | tf_op jit(solution)/shard_map/pallas_call | solution.py:865
